TPU v7x, 256 devices: a whole 4x4x8 slice. The times are simulated.
256 devices in a mesh: seq: 64 (over z, x, core), dp: 4 (over y).
Axes of the slice: x: 4, y: 4, z: 8, core: 2. Of those that a mesh axis runs over, the one named last changes fastest.
Arguments:
- conv_input: bfloat16 [4, 16384, 256], P('dp', 'seq'), may hold values from -6 to 6
- in_state_map: bfloat16 [4, 16384, 128], P('dp', 'seq'), may hold values from -6 to 6
- out_state_map: bfloat16 [4, 16384, 128], P('dp', 'seq'), may hold values from -1.25 to 1.25
- step_size: float32 [4, 16384, 4], P('dp', 'seq'), may hold values from 0.01 to 0.1
- decay_rate: float32 [4], replicated, may hold values from 0.00030517578 to 1.3
- skip_gain: float32 [4], replicated, may hold values from 0.5 to 1.5
- conv_weight: float32 [4, 256], replicated, may hold values from -3 to 3
- grad_mixer: bfloat16 [4, 16384, 256], P('dp', 'seq'), may hold values from -6 to 6
- grad_output: bfloat16 [4, 16384, 8192], P('dp', 'seq'), may hold values from -0.15625 to 0.15625
Outputs:
- grad_conv_input: bfloat16 [4, 16384, 256], P('dp', 'seq')
- grad_in_map: bfloat16 [4, 16384, 128], P('dp', 'seq')
- grad_out_map: bfloat16 [4, 16384, 128], P('dp', 'seq')
- grad_conv_weight: float32 [4, 256], replicated
- grad_out_proj: float32 [8192, 256], P(('seq', 'dp'))
All inputs are finite; a program needn't handle non-finite values.
Results may differ from a plain program's by a relative error of at most 0.009.
Values may be sent and summed in bfloat16 or wider, within the bound.
A program may use at most 64 MiB of HBM per device.

v0:
```python
import functools

import jax
import jax.numpy as jnp
from jax import lax
from jax.sharding import Mesh
from jax.sharding import PartitionSpec as P

SEQ = ("seq_0", "seq_1", "seq_2")
SEQ_DP = ("seq_0", "seq_1", "seq_2", "dp")


highest = lax.Precision.HIGHEST


def shifted(value, axis, by):
    size = lax.axis_size(axis)
    pairs = [(i, i + by) for i in range(size) if 0 <= i + by < size]
    return lax.ppermute(value, axis, pairs)


def laid_out(pieces, dim):
    pieces = jnp.moveaxis(pieces, 0, dim)
    shape = pieces.shape
    return pieces.reshape(*shape[:dim], shape[dim] * shape[dim + 1], *shape[dim + 2 :])


def copy_for_each(value, axis):
    size = lax.axis_size(axis)
    return lax.all_to_all(
        jnp.broadcast_to(value[None], (size, *value.shape)), axis, 0, 0, tiled=True
    )


def gather_directly(value, axis, dim):
    return laid_out(copy_for_each(value, axis), dim)


def side_by_side(arrays, axis, dim, along):
    ends, at = ([], 0)
    for a in arrays[:-1]:
        at += a.shape[along]
        ends.append(at)
    both = jnp.concatenate(arrays, axis=along)
    return tuple(jnp.split(lax.all_gather(both, axis, axis=dim, tiled=True), ends, axis=along))


def one_axis_at_a_time(value, axes):
    return functools.reduce(lax.psum, axes, value)


def reduced_to_own(pieces, axes, order):
    inside = pieces.shape[1:]
    pieces = pieces.reshape(*(lax.axis_size(a) for a in axes), *inside)
    pieces = jnp.moveaxis(pieces, order, range(len(axes))).reshape(-1, *inside)
    for k in order:
        pieces = lax.psum_scatter(pieces, axes[k], scatter_dimension=0, tiled=True)
    return pieces[0]


def cut_along(value, dim, size):
    before, after = (value.shape[:dim], value.shape[dim + 1 :])
    return jnp.moveaxis(value.reshape(*before, size, -1, *after), dim, 0)


def summed_rows(value, axes, order, dim):
    size = lax.axis_size(axes)
    return reduced_to_own(cut_along(value, dim, size), axes, order)


def product(left_side, right_side):
    return jnp.dot(left_side, right_side, precision=highest, preferred_element_type=jnp.float32)


def lowdot(left_side, right_side, left_dim, right_dim):
    return lax.dot_general(
        left_side,
        right_side,
        (((left_dim,), (right_dim,)), ((), ())),
        preferred_element_type=jnp.float32,
    )


def silu_slope(pre_act):
    gate_value = jax.nn.sigmoid(pre_act)
    return gate_value * (1.0 + pre_act * (1.0 - gate_value))


def head_terms(
    source_head,
    upstream,
    decay_sums,
    step_rows,
    start_state,
    end_grad,
    skip_head,
    scores,
    in_map,
    out_map,
    in_wide,
    out_wide,
):
    length = decay_sums.shape[0]
    places = jnp.arange(length)
    causal = places[:, None] >= places[None, :]
    spread = decay_sums[:, None] - decay_sums[None, :]
    segment = jnp.where(causal, jnp.exp(jnp.where(causal, spread, 0.0)), 0.0)
    mixing = (segment * scores * step_rows[None, :]).astype(jnp.bfloat16)
    source_wide = source_head.astype(jnp.float32)
    upstream_wide = upstream.astype(jnp.float32)
    leading = jnp.exp(decay_sums)
    trailing = jnp.exp(decay_sums[-1] - decay_sums)
    output = (
        lowdot(mixing, source_head, 1, 0)
        + leading[:, None] * product(out_wide, start_state.T)
        + skip_head * source_wide
    )
    grad_source = (
        lowdot(mixing, upstream, 0, 0)
        + (step_rows * trailing)[:, None] * product(in_wide, end_grad.T)
        + skip_head * upstream_wide
    )
    pairing = lowdot(upstream, source_head, 1, 1)
    weighted = (segment * step_rows[None, :] * pairing).astype(jnp.bfloat16)
    grad_in = lowdot(weighted, out_map, 0, 0) + (step_rows * trailing)[:, None] * product(
        source_wide, end_grad
    )
    grad_out = lowdot(weighted, in_map, 1, 0) + leading[:, None] * product(
        upstream_wide, start_state
    )
    return (output, grad_source, grad_in, grad_out)


def block_carries(source, upstream, decay_sums, step_rows, in_wide, out_wide):
    remaining = jnp.exp(decay_sums[-1][None, :] - decay_sums)
    weighted_source = source.astype(jnp.float32) * (step_rows * remaining)[:, :, None]
    state_part = jnp.einsum("lhp,ln->hpn", weighted_source, in_wide, precision=highest)
    weighted_grad = upstream.astype(jnp.float32) * jnp.exp(decay_sums)[:, :, None]
    grad_part = jnp.einsum("lhp,ln->hpn", weighted_grad, out_wide, precision=highest)
    return (state_part, grad_part)


def block_terms(
    source, upstream, decay_sums, step_rows, in_map, out_map, start_states, end_grads, skip_gain
):
    scores = jnp.dot(out_map, in_map.T, preferred_element_type=jnp.float32)
    in_wide = in_map.astype(jnp.float32)
    out_wide = out_map.astype(jnp.float32)

    def one_head(head_items):
        return head_terms(
            head_items[0],
            head_items[1],
            head_items[2],
            head_items[3],
            head_items[4],
            head_items[5],
            head_items[6],
            scores,
            in_map,
            out_map,
            in_wide,
            out_wide,
        )

    outputs, grad_source, grad_in, grad_out = lax.map(
        one_head,
        (
            source.transpose(1, 0, 2),
            upstream.transpose(1, 0, 2),
            decay_sums.T,
            step_rows.T,
            start_states,
            end_grads,
            skip_gain,
        ),
    )
    length = source.shape[0]
    outputs = outputs.transpose(1, 0, 2).reshape(length, -1)
    grad_source = grad_source.transpose(1, 0, 2).reshape(length, -1)
    return (outputs, grad_source, jnp.sum(grad_in, 0), jnp.sum(grad_out, 0))


def on_device(
    conv_input,
    in_state_map,
    out_state_map,
    step_size,
    decay_rate,
    skip_gain,
    conv_weight,
    grad_mixer,
    grad_output,
):
    tap_count = conv_weight.shape[0]
    tokens = conv_input.shape[1]
    channels = conv_input.shape[2]
    head_count = decay_rate.shape[0]
    head_size = channels // head_count
    local_input = conv_input[0]
    before = shifted(local_input[tokens - (tap_count - 1) :], SEQ, 1)
    extended = jnp.concatenate([before, local_input], 0).astype(jnp.float32)
    pre_act = jnp.zeros((tokens, channels), jnp.float32)
    for offset in range(tap_count):
        pre_act = (
            pre_act
            + conv_weight[offset]
            * extended[tap_count - 1 - offset : tap_count - 1 - offset + tokens]
        )
    source = jax.nn.silu(pre_act).astype(jnp.bfloat16)
    step_rows = step_size[0]
    decay_sums = jnp.cumsum(-step_rows * decay_rate[None, :], axis=0)
    source_heads = source.reshape(tokens, head_count, head_size)
    upstream = grad_mixer[0].reshape(tokens, head_count, head_size)
    in_map = in_state_map[0]
    out_map = out_state_map[0]
    state_part, grad_part = block_carries(
        source_heads,
        upstream,
        decay_sums,
        step_rows,
        in_map.astype(jnp.float32),
        out_map.astype(jnp.float32),
    )
    totals = gather_directly(decay_sums[-1:], SEQ, 0)
    ranks = totals.shape[0]
    before_sums = jnp.cumsum(totals, axis=0) - totals
    own_rank = lax.axis_index(SEQ)
    position = jnp.arange(ranks)
    own_row = (position == own_rank).astype(jnp.float32)
    own_start = product(own_row[None, :], before_sums)[0]
    own_end = own_start + product(own_row[None, :], totals)[0]
    pieces = side_by_side((state_part[None], grad_part[None]), SEQ, 0, 1)
    piece_count = pieces[0].shape[0]
    indices = jnp.arange(piece_count)
    selector = (indices[:, None] == position[None, :]).astype(jnp.float32)
    piece_start = product(selector, before_sums)
    piece_end = piece_start + product(selector, totals)
    earlier = (indices < own_rank)[:, None]
    after_own = (indices > own_rank)[:, None]
    forward_weight = jnp.where(
        earlier, jnp.exp(jnp.where(earlier, own_start[None, :] - piece_end, 0.0)), 0.0
    )
    backward_weight = jnp.where(
        after_own, jnp.exp(jnp.where(after_own, piece_start - own_end[None, :], 0.0)), 0.0
    )
    start_state = jnp.einsum("kh,khpn->hpn", forward_weight, pieces[0], precision=highest)
    end_grad = jnp.einsum("kh,khpn->hpn", backward_weight, pieces[1], precision=highest)
    outputs, grad_source, grad_in, grad_out = block_terms(
        source_heads,
        upstream,
        decay_sums,
        step_rows,
        in_map,
        out_map,
        start_state,
        end_grad,
        skip_gain,
    )
    mixer_out = outputs.astype(jnp.bfloat16)
    grad_pre = grad_source * silu_slope(pre_act)
    following = shifted(grad_pre[: tap_count - 1], SEQ, -1)
    padded = jnp.concatenate([grad_pre, following], 0)
    grad_input = jnp.zeros((tokens, channels), jnp.float32)
    for offset in range(tap_count):
        grad_input = grad_input + conv_weight[offset] * padded[offset : offset + tokens]
    weight_terms = jnp.stack(
        [
            jnp.sum(
                grad_pre * extended[tap_count - 1 - offset : tap_count - 1 - offset + tokens], 0
            )
            for offset in range(tap_count)
        ]
    )
    token_total = tokens * lax.axis_size(SEQ) * lax.axis_size("dp")
    grad_weight = one_axis_at_a_time(weight_terms, SEQ_DP) * float(token_total) ** (-0.5)
    local_grad = grad_output[0]
    proj_grad = summed_rows(
        lax.dot_general(
            local_grad, mixer_out, (((0,), (0,)), ((), ())), preferred_element_type=jnp.float32
        ),
        SEQ_DP,
        (2, 0, 1, 3),
        0,
    )
    return (
        grad_input.astype(jnp.bfloat16)[None],
        grad_in.astype(jnp.bfloat16)[None],
        grad_out.astype(jnp.bfloat16)[None],
        grad_weight,
        proj_grad,
    )


def solution(mesh):
    torus = Mesh(mesh.devices.reshape(8, 4, 2, mesh.shape["dp"]), ("seq_0", "seq_1", "seq_2", "dp"))
    return jax.shard_map(
        on_device,
        mesh=torus,
        in_specs=(
            P("dp", SEQ, None),
            P("dp", SEQ, None),
            P("dp", SEQ, None),
            P("dp", SEQ, None),
            P(),
            P(),
            P(),
            P("dp", SEQ, None),
            P("dp", SEQ, None),
        ),
        out_specs=(
            P("dp", SEQ, None),
            P("dp", SEQ, None),
            P("dp", SEQ, None),
            P(),
            P(SEQ_DP, None),
        ),
        check_vma=False,
    )
```

profile of v0, /device:TPU:2, one launch (start us, length us, event | category | flops | bytes accessed | tf_op | source)
XLA Modules:
  0.0 340.6 jit_solution(3425074739502957284)
XLA Ops:
  7.2 1.0 copy.43
  8.3 1.9 collective-permute-start
  11.0 1.2 reduce-window.6
  14.4 1.0 copy.46
  15.5 1.1 convolution_bitcast_fusion.1
  17.2 1.1 convolution_bitcast_fusion.2
  19.6 12.9 %all-to-all-start = ((f32[64,1,4]{2,1,0:T(1,128)}), f32[64,1,4]{2,1,0:T(1,128)S(1)}, u32[]{:S(2)}, u32[]{:S(2)}) async-start(f32[64,1,4]{2,1,0:T(1,128)} %broadcast_in_dim.86), calls=%async_computation | async-start | bytes 65536 | tf_op jit(solution)/shard_map/all_to_all | solution.py:30
  32.6 0.9 bitcast_convert_fusion
  33.5 1.1 fusion.77
  34.6 6.5 %all-to-all-done = f32[64,1,4]{2,1,0:T(1,128)S(1)} async-done(((f32[64,1,4]{2,1,0:T(1,128)}), f32[64,1,4]{2,1,0:T(1,128)S(1)}, u32[]{:S(2)}, u32[]{:S(2)}) %all-to-all-start) | async-done | bytes 1056 | tf_op jit(solution)/shard_map/all_to_all | solution.py:30
  41.9 79.1 %all-gather.2.cloned.1.call-done = f32[64,8,64,128]{3,2,1,0:T(8,128)} async-done(((f32[1,8,64,128]{3,2,1,0:T(8,128)}), f32[64,8,64,128]{3,2,1,0:T(8,128)}) %all-gather.2.cloned.1.call-update) | async-done | bytes 16777232 | tf_op jit(solution)/shard_map/all_gather | solution.py:45
  121.0 6.9 %fusion.81 = (f32[64,4,64,128]{3,2,1,0:T(8,128)S(1)}, f32[64,4,64,128]{3,2,1,0:T(8,128)S(1)}) fusion(f32[64,8,64,128]{3,2,1,0:T(8,128)} %all-gather.2.cloned.1.call-done), kind=kLoop, calls=%fused_computation.136 | loop fusion | bytes 33554432 | tf_op jit(solution)/shard_map/split | solution.py:45
  128.0 8.6 %fusion.44 = f32[4,1,64,128]{3,1,2,0:T(1,128)S(1)} fusion(f32[64,4,1,1]{0,2,3,1:T(1,128)S(1)} %bitcast.294, f32[64,4,64,128]{3,2,1,0:T(8,128)S(1)} %get-tuple-element.161), kind=kOutput, calls=%fused_computation.59 | convolution fusion | flops 25165824 | bytes 8520704 | tf_op jit(solution)/shard_map/kh,khpn->hpn/dot_general | solution.py:247
  136.6 8.8 %fusion.42 = f32[4,1,64,128]{3,1,2,0:T(1,128)S(1)} fusion(f32[64,4,1,1]{0,2,3,1:T(1,128)S(1)} %bitcast.288, f32[64,4,64,128]{3,2,1,0:T(8,128)S(1)} %get-tuple-element.160), kind=kOutput, calls=%fused_computation.57 | convolution fusion | flops 25165824 | bytes 8520704 | tf_op jit(solution)/shard_map/kh,khpn->hpn/dot_general | solution.py:248
  145.4 24.4 %while.16 = (s32[]{:T(128)}, bf16[4,256,64]{1,2,0:T(8,128)(2,1)S(1)}, f32[4,256,64]{1,2,0:T(8,128)S(1)}, f32[4,256,128]{2,1,0:T(8,128)S(1)}, f32[4,256,128]{2,1,...) while((s32[]{:T(128)}, ...), condition=%wide.region_4.5_spmd, body=%wide.region_3.4_spmd.sunk | while | flops 161055232 | bytes 2911473 | solution.py:166
  149.4 0.9 fusion.138
  150.6 0.9 fusion.136
  155.5 0.9 fusion.138
  156.7 0.9 fusion.136
  162.8 0.9 fusion.136
  168.9 0.9 fusion.136
  169.8 6.7 %convolution_bitcast_fusion = f32[8192,256]{0,1:T(8,128)} fusion(bf16[256,256]{0,1:T(8,128)(2,1)S(1)} %bitcast.266, bf16[1,256,8192]{2,1,0:T(8,128)(2,1)} %param.19), kind=kOutput, calls=%fused_computation.56 | convolution fusion | flops 1073741824 | bytes 12713984 | tf_op jit(solution)/shard_map/dot_general | solution.py:279
  176.5 9.0 %copy.48 = f32[8192,256]{1,0:T(8,128)} copy(f32[8192,256]{0,1:T(8,128)} %convolution_bitcast_fusion) | data formatting | bytes 16777216 | tf_op jit(solution)/shard_map/dot_general | solution.py:279
  185.5 8.3 %copy.49 = f32[2,8,4,4,32,256]{5,4,3,2,1,0:T(8,128)} copy(f32[2,8,4,4,32,256]{5,4,3,0,2,1:T(8,128)} %bitcast.251) | data formatting | bytes 16777216 | tf_op jit(solution)/shard_map/transpose | solution.py:55
  193.8 20.2 %reduce-scatter.5.cloned.1.call-done = f32[128,32,256]{2,1,0:T(8,128)} async-done(((f32[256,32,256]{2,1,0:T(8,128)}), f32[128,32,256]{2,1,0:T(8,128)}) %reduce-scatter.5.cloned.1.call-update) | async-done | bytes 4194320 | tf_op jit(solution)/shard_map/reduce_scatter | solution.py:57
  214.1 59.1 %reduce-scatter.7.cloned.1.call-done = f32[16,32,256]{2,1,0:T(8,128)} async-done(((f32[128,32,256]{2,1,0:T(8,128)}), f32[16,32,256]{2,1,0:T(8,128)}) %reduce-scatter.7.cloned.1.call-update) | async-done | bytes 524304 | tf_op jit(solution)/shard_map/reduce_scatter | solution.py:57
  273.7 1.9 collective-permute-start.1
  275.7 15.5 %psum.28 = f32[4,256]{1,0:T(4,128)S(1)} all-reduce(f32[4,256]{1,0:T(4,128)S(1)} %pad_maximum_fusion.2), channel_id=1, replica_groups=mesh['seq_0'=8,'seq_1'=4,'seq_2'=2,'dp'=4] {'seq_0'}, use_global_device_ids=true, to_apply=%region_11.12 | all-reduce | flops 1024 | bytes 8192 | tf_op jit(solution)/shard_map/psum | solution.py:49
  291.2 11.1 %psum.29 = f32[4,256]{1,0:T(4,128)S(1)} all-reduce(f32[4,256]{1,0:T(4,128)S(1)} %psum.28), channel_id=1, replica_groups=mesh['seq_0'=8,'seq_1'=4,'seq_2'=2,'dp'=4] {'seq_1'}, use_global_device_ids=true, to_apply=%region_12.13 | all-reduce | flops 1024 | bytes 8192 | tf_op jit(solution)/shard_map/psum | solution.py:49
  302.4 2.5 psum.30
  304.8 10.4 %psum.31 = f32[4,256]{1,0:T(4,128)S(1)} all-reduce(f32[4,256]{1,0:T(4,128)S(1)} %psum.30), channel_id=1, replica_groups=mesh['seq_0'=8,'seq_1'=4,'seq_2'=2,'dp'=4] {'dp'}, use_global_device_ids=true, to_apply=%region_14.15 | all-reduce | flops 1024 | bytes 8192 | tf_op jit(solution)/shard_map/psum | solution.py:49
  318.5 15.6 %reduce-scatter.11.cloned.1.call-done = f32[1,32,256]{2,1,0:T(8,128)} async-done(((f32[4,32,256]{2,1,0:T(8,128)}), f32[1,32,256]{2,1,0:T(8,128)}) %reduce-scatter.11.cloned.1.call-update) | async-done | bytes 32784 | tf_op jit(solution)/shard_map/reduce_scatter | solution.py:57
  (101 shorter events, 28.3 us)
Async XLA Ops:
  7.2 113.8 %all-gather.2.cloned.1.call-start = ((), (), s32[]{:S(2)}) async-start(), calls=%async_computation.5 | async-start | bytes 17039360 | tf_op jit(solution)/shard_map/all_gather | solution.py:45
  8.3 8.3 %collective-permute-start = (bf16[3,256]{0,1:T(8,128)(2,1)S(1)}, bf16[3,256]{0,1:T(8,128)(2,1)S(1)}, u32[]{:S(2)}, u32[]{:S(2)}) collective-permute-start(bf16[3,256]{0,1:T(8,128)(2,1)S(1)} %slice_bitcast_fusion), channel_id=1, source_target_pairs={{0,4},{4,8},{8,12},{12,16},{16,20},{20,24},{24,28},{28,32},{32,36}... | collective-permute-start | bytes 4616 | tf_op jit(solution)/shard_map/ppermute | solution.py:19
  19.6 21.5 %all-to-all-start = ((f32[64,1,4]{2,1,0:T(1,128)}), f32[64,1,4]{2,1,0:T(1,128)S(1)}, u32[]{:S(2)}, u32[]{:S(2)}) async-start(f32[64,1,4]{2,1,0:T(1,128)} %broadcast_in_dim.86), calls=%async_computation | async-start | bytes 65536 | tf_op jit(solution)/shard_map/all_to_all | solution.py:30
  32.6 181.4 %reduce-scatter.5.cloned.1.call-start = ((), (), s32[]{:S(2)}) async-start(), calls=%async_computation.6 | async-start | bytes 12582912 | tf_op jit(solution)/shard_map/reduce_scatter | solution.py:57
  127.9 17.5 %copy-start = (bf16[1,256,128]{2,1,0:T(8,128)(2,1)S(1)}, bf16[1,256,128]{2,1,0:T(8,128)(2,1)}, u32[]{:S(2)}) copy-start(bf16[1,256,128]{2,1,0:T(8,128)(2,1)} %param.12) | copy-start | bytes 196612
  127.9 17.4 %copy-start.1 = (bf16[1,256,128]{2,1,0:T(8,128)(2,1)S(1)}, bf16[1,256,128]{2,1,0:T(8,128)(2,1)}, u32[]{:S(2)}) copy-start(bf16[1,256,128]{2,1,0:T(8,128)(2,1)} %param.13) | copy-start | bytes 196612
  128.0 17.4 %copy-start.2 = (f32[4]{0:T(128)S(1)}, f32[4]{0:T(128)}, u32[]{:S(2)}) copy-start(f32[4]{0:T(128)} %param.16) | copy-start | bytes 52
  193.8 79.4 %reduce-scatter.7.cloned.1.call-start = ((), (), s32[]{:S(2)}) async-start(), calls=%async_computation.7 | async-start | bytes 4718592 | tf_op jit(solution)/shard_map/reduce_scatter | solution.py:57
  214.0 101.3 %reduce-scatter.9.cloned.1.call-start = ((), (), s32[]{:S(2)}) async-start(), calls=%async_computation.8 | async-start | bytes 655360 | tf_op jit(solution)/shard_map/reduce_scatter | solution.py:57
  273.2 60.9 %reduce-scatter.11.cloned.1.call-start = ((), (), s32[]{:S(2)}) async-start(), calls=%async_computation.9 | async-start | bytes 163840 | tf_op jit(solution)/shard_map/reduce_scatter | solution.py:57
  273.7 43.5 %collective-permute-start.1 = (f32[3,256]{0,1:T(8,128)S(1)}, f32[3,256]{0,1:T(8,128)S(1)}, u32[]{:S(2)}, u32[]{:S(2)}) collective-permute-start(f32[3,256]{0,1:T(8,128)S(1)} %slice.88), channel_id=1, source_target_pairs={{4,0},{8,4},{12,8},{16,12},{20,16},{24,20},{28,24},{32,28},{36,32}... | collective-permute-start | bytes 9224 | tf_op jit(solution)/shard_map/ppermute | solution.py:19
Sparse Core Ops, SparseCore 0:
  19.1 101.8 all-gather.1
  193.9 20.0 reduce-scatter.4
  216.6 56.5 reduce-scatter.6
  275.6 20.7 reduce-scatter.8
  315.4 18.5 reduce-scatter.10
where the time goes:
time: 342 us; the launch traced here: 341 us
  waiting for transfers between devices  181 us (53%)
  matrix products  42.1 us (12%)
  blocking collectives  39.6 us (12%)
  local copies, waits for them, and re-layouts  36.5 us (11%)
  starting transfers between devices  17 us (5%)
  between operations  14 us (4%)
  other arithmetic  10.6 us (3%)
    reduce_scatter x4, waiting for transfers between devices, reduced_to_own(): pieces = lax.psum_scatter(pieces, axes[k], scatter_dimension=0, tiled=True)  94.9 us
    all_gather x1, waiting for transfers between devices, side_by_side(): lax.all_gather(both, axis, axis=dim, tiled=True)  79.1 us
    psum x4, blocking collectives, one_axis_at_a_time(): return functools.reduce(lax.psum, axes, value)  39.6 us
    all_to_all x1, starting transfers between devices, copy_for_each(): lax.all_to_all(jnp.broadcast_to(value[None], (size, *value.shape)), axis,...  12.9 us
    dot_general x1, local copies, waits for them, and re-layouts, on_device(): lax.dot_general(local_grad, mixer_out, (((0,), (0,)), ((), ())), preferre...  9 us
    dot_general x1, matrix products, on_device(): jnp.einsum('kh,khpn->hpn', backward_weight, pieces[1], precision=highest)  8.82 us
    dot_general x1, matrix products, on_device(): jnp.einsum('kh,khpn->hpn', forward_weight, pieces[0], precision=highest)  8.59 us
    transpose x1, local copies, waits for them, and re-layouts, reduced_to_own(): pieces = jnp.moveaxis(pieces, order, range(len(axes))).reshape(-1, *inside)  8.25 us
  transfers between devices with their start and end apart: 8, of which 5 were waited for; matrix products, arithmetic and copies ran while one was open for 4% of the time, Pallas kernels for 0%

commit v1 on v0

v1 whole, which is shorter than its diff:
```python
import jax
import jax.numpy as jnp
from jax import lax
from jax.experimental import pallas as pl
from jax.experimental.pallas import tpu as pltpu
from jax.sharding import PartitionSpec as P

MESH = pl.DeviceIdType.MESH
F32 = jnp.float32
BF16 = jnp.bfloat16

NZ, NX, NC, NY = 8, 4, 2, 4
ROW = NX * NC
HEADS, HEAD_DIM, STATE = 4, 64, 128
TOK, INNER, TAPS = 256, 256, 4
SCALE = float(TOK * NZ * NX * NC * NY) ** -0.5
ORDER = (
    (2, 0), (0, 2), (2, 1), (1, 2), (2, 2), (2, 3), (3, 2), (1, 3),
    (3, 1), (3, 0), (0, 3), (1, 0), (0, 1), (1, 1), (3, 3), (0, 0),
)


class Counter:
    def __init__(self):
        self.used = 0

    def take(self, count=1):
        first = self.used
        self.used += count
        return first


def dot(a, b, da, db):
    return lax.dot_general(a, b, (((da,), (db,)), ((), ())), preferred_element_type=F32)


def exact(a, b, da, db):
    return lax.dot_general(
        a,
        b,
        (((da,), (db,)), ((), ())),
        precision=lax.Precision.HIGHEST,
        preferred_element_type=F32,
    )


def scan_slot(place, size, core):
    return place + core * (size - 1 - 2 * place)


def kernel(
    x_ref, b_ref, c_ref, step_ref, rate_ref, skip_ref, taps_ref, up_ref, g_ref,
    out_x, out_b, out_c, out_w, out_p,
    halo, ext, pre, src, ws, wg, lead, trail,
    tot, pieces, row_p, row_t, prefix, row_sum, row_log, z_p, z_t, z_state, back, states,
    loc_out, loc_src, loc_b, loc_c, mix, mix_peer,
    g_own, g_peer, gt,
    acc0, hold1, hold3, send2, relay, send1, send3, from_m, from_p, acc1, send_b, recv_b,
    part3, send_z, recv_z, grad_pre, w_row, w_y, w_z,
    g_sem, ssem, rsem,
):
    s = lax.axis_index("seq")
    y = lax.axis_index("dp")
    core = lax.rem(s, 2)
    x = lax.rem(lax.div(s, 2), 4)
    z = lax.div(s, ROW)
    j = lax.rem(s, ROW)
    count = Counter()
    waits = []

    def send(source, target, to, index, slot=None):
        copy = pltpu.make_async_remote_copy(
            src_ref=source,
            dst_ref=target,
            send_sem=ssem.at[index],
            recv_sem=rsem.at[index if slot is None else slot],
            device_id=to,
            device_id_type=MESH,
        )
        copy.start()
        return copy

    def arrived(target, slot):
        pltpu.make_async_remote_copy(
            src_ref=target,
            dst_ref=target,
            send_sem=ssem.at[0],
            recv_sem=rsem.at[slot],
            device_id=(s, y),
            device_id_type=MESH,
        ).wait_recv()

    def row_mate(d):
        other = lax.rem(j + d, ROW)
        return other, (z * ROW + other, y)

    def at_x(d):
        return ((z * NX + lax.rem(x + d, NX)) * NC + core, y)

    def at_y(d):
        return (s, lax.rem(y + d, NY))

    def at_z(d):
        other = lax.rem(z + d, NZ)
        return other, (other * ROW + j, y)

    peer = (s + 1 - 2 * core, y)
    following = (lax.rem(s + 1, NZ * ROW), y)
    previous = (lax.rem(s + NZ * ROW - 1, NZ * ROW), y)

    barrier = pltpu.get_barrier_semaphore()
    partners = [row_mate(d)[1] for d in range(1, ROW)]
    partners += [at_z(d)[1] for d in range(1, NZ)]
    partners += [at_y(d) for d in range(1, NY)]
    partners += [following, previous]
    for partner in partners:
        pl.semaphore_signal(barrier, inc=1, device_id=partner, device_id_type=MESH)

    @pl.loop(0, NZ * NX)
    def _(i):
        at = pl.multiple_of((i * NC + core) * 128, 128)
        pltpu.make_async_copy(g_ref.at[0, :, pl.ds(at, 128)], g_own.at[i], g_sem.at[0]).start()

    steps = step_ref[...]
    head_row = lax.broadcasted_iota(jnp.int32, (HEADS, TOK), 0)
    rates = jnp.full((HEADS, TOK), rate_ref[0], F32)
    for h in range(1, HEADS):
        rates = jnp.where(head_row == h, rate_ref[h], rates)
    token_r = lax.broadcasted_iota(jnp.int32, (TOK, TOK), 0)
    token_c = lax.broadcasted_iota(jnp.int32, (TOK, TOK), 1)
    upper = jnp.where(token_r <= token_c, 1.0, 0.0).astype(F32)
    sums = exact(-steps * rates, upper, 1, 0)
    rows = jnp.concatenate([sums, steps], axis=0)
    cols = rows.T
    head_of = lax.div(lax.broadcasted_iota(jnp.int32, (8, INNER), 1), HEAD_DIM)
    row_of = lax.broadcasted_iota(jnp.int32, (8, INNER), 0)
    sums_wide = exact(rows, jnp.where(row_of == head_of, 1.0, 0.0).astype(F32), 0, 0)
    step_wide = exact(rows, jnp.where(row_of == head_of + HEADS, 1.0, 0.0).astype(F32), 0, 0)
    lead[...] = jnp.exp(sums_wide)
    trail[...] = step_wide * jnp.exp(sums_wide[TOK - 1 : TOK, :] - sums_wide)
    tot[...] = jnp.broadcast_to(rows[:, TOK - 1 : TOK], (8, 128))
    upstream = up_ref[0]
    in_map = b_ref[0]
    out_map = c_ref[0]
    wg[...] = (upstream.astype(F32) * lead[...]).astype(BF16)
    grad_piece = dot(wg[...], out_map, 0, 0).astype(BF16)
    for h in range(HEADS):
        pieces[1, h] = grad_piece[h * HEAD_DIM : (h + 1) * HEAD_DIM]
    ext[16:, :] = x_ref[0].astype(F32)

    pl.semaphore_wait(barrier, len(partners))

    k = count.take()
    waits.append(send(x_ref.at[0, pl.ds(TOK - 16, 16), :], halo, following, k))

    slot_j = [scan_slot(j, ROW, c) for c in range(NC)]
    my_slot = scan_slot(j, ROW, core)
    total_at = count.take(ROW)
    row_t[my_slot] = tot[...]
    for d in range(1, ROW):
        other, to = row_mate(d)
        slot = scan_slot(j, ROW, lax.rem(other, 2))
        waits.append(send(tot, row_t.at[slot], to, total_at + d, total_at + slot))

    @pl.loop(0, NZ * NX)
    def _(i):
        at = pl.multiple_of((i * NC + 1 - core) * 128, 128)
        pltpu.make_async_remote_copy(
            src_ref=g_ref.at[0, :, pl.ds(at, 128)],
            dst_ref=g_peer.at[i],
            send_sem=g_sem.at[1],
            recv_sem=g_sem.at[2],
            device_id=peer,
            device_id_type=MESH,
        ).start()

    arrived(halo, k)
    first = jnp.where(s > 0, 1.0, 0.0)
    ext[0:16, :] = halo[...].astype(F32) * first
    value = jnp.zeros((TOK, INNER), F32)
    for tap in range(TAPS):
        value = value + taps_ref[tap : tap + 1, :] * ext[16 - tap : 16 - tap + TOK, :]
    pre[...] = value
    source = (value * jax.nn.sigmoid(value)).astype(BF16)
    src[...] = source
    ws[...] = (source.astype(F32) * trail[...]).astype(BF16)
    state_piece = dot(ws[...], in_map, 0, 0).astype(BF16)
    for h in range(HEADS):
        pieces[0, h] = state_piece[h * HEAD_DIM : (h + 1) * HEAD_DIM]

    piece_at = count.take(ROW)
    row_p[my_slot] = pieces[core, x]
    for d in range(1, ROW):
        other, to = row_mate(d)
        theirs = lax.rem(other, 2)
        slot = scan_slot(j, ROW, theirs)
        waits.append(
            send(pieces.at[theirs, lax.div(other, 2)], row_p.at[slot], to, piece_at + d, piece_at + slot)
        )

    scores = dot(out_map, in_map, 1, 1)
    causal = token_r >= token_c
    low = lax.broadcasted_iota(jnp.int32, (TOK, 128), 1) < HEAD_DIM
    for pair in range(HEADS // 2):
        lanes = slice(pair * 128, (pair + 1) * 128)
        sp = src[:, lanes]
        upp = up_ref[0, :, lanes]
        outs, grads = [], []
        for half in range(2):
            h = 2 * pair + half
            mine = low if half == 0 else jnp.logical_not(low)
            spread = cols[:, h : h + 1] - rows[h : h + 1, :]
            seg = jnp.where(causal, jnp.exp(jnp.where(causal, spread, 0.0)), 0.0)
            seg = seg * rows[HEADS + h : HEADS + h + 1, :]
            mixing = (seg * scores).astype(BF16)
            outs.append(dot(mixing, sp, 1, 0))
            grads.append(dot(mixing, upp, 0, 0))
            up_only = jnp.where(mine, upp.astype(F32), 0.0).astype(BF16)
            weighted = (seg * dot(up_only, sp, 1, 1)).astype(BF16)
            part_b = dot(weighted, out_map, 0, 0)
            part_c = dot(weighted, in_map, 1, 0)
            if h == 0:
                loc_b[...] = part_b
                loc_c[...] = part_c
            else:
                loc_b[...] += part_b
                loc_c[...] += part_c
        gain = jnp.where(low, skip_ref[2 * pair], skip_ref[2 * pair + 1])
        loc_out[:, lanes] = jnp.where(low, outs[0], outs[1]) + gain * sp.astype(F32)
        loc_src[:, lanes] = jnp.where(low, grads[0], grads[1]) + gain * upp.astype(F32)

    for d in range(1, ROW):
        slot = scan_slot(lax.rem(j + ROW - d, ROW), ROW, core)
        arrived(row_t.at[slot], total_at + slot)
        arrived(row_p.at[slot], piece_at + slot)
    running = jnp.zeros((HEAD_DIM, STATE), F32)
    decayed = jnp.zeros((1, 128), F32)
    before = []
    for q in range(ROW):
        prefix[q] = running
        before.append(decayed)
        own = row_t[q, pl.ds(x, 1), :]
        running = jnp.exp(own) * running + row_p[q].astype(F32)
        decayed = decayed + own
    row_sum[...] = running.astype(BF16)
    row_log[...] = jnp.broadcast_to(decayed, (8, 128))

    my_z = scan_slot(z, NZ, core)
    zs_at = count.take(NZ)
    zl_at = count.take(NZ)
    z_copies = []
    for d in range(1, NZ):
        other, to = at_z(d)
        later = scan_slot(other, NZ, core) > my_z
        pair_of = [
            pltpu.make_async_remote_copy(
                src_ref=source,
                dst_ref=target.at[my_z],
                send_sem=ssem.at[base + d],
                recv_sem=rsem.at[base + my_z],
                device_id=to,
                device_id_type=MESH,
            )
            for source, target, base in ((row_log, z_t, zl_at), (row_sum, z_p, zs_at))
        ]
        z_copies.append((later, pair_of))

        @pl.when(later)
        def _(pair_of=pair_of):
            for copy in pair_of:
                copy.start()

    def turned(held, column):
        @pl.loop(0, NZ * NX)
        def _(i):
            xi = lax.rem(i, NX)
            zi = pl.multiple_of(lax.div(i, NX) * 32, 32)
            block = held[i].T
            for yi in range(NY):
                gt[xi, yi, pl.ds(zi, 32), column : column + TOK] = block[yi * 32 : (yi + 1) * 32]

    pltpu.make_async_copy(g_own, g_own, g_sem.at[0]).wait()
    turned(g_own, 0)

    z_state[...] = jnp.zeros_like(z_state)
    for q in range(NZ - 1):

        @pl.when(q < my_z)
        def _(q=q):
            arrived(z_t.at[q], zl_at + q)
            arrived(z_p.at[q], zs_at + q)
            z_state[...] = jnp.exp(z_t[q, 0:1, :]) * z_state[...] + z_p[q].astype(F32)

    entering = z_state[...]
    for q in range(ROW):
        back[q] = (jnp.exp(before[q]) * entering + prefix[q]).astype(BF16)
    back_at = count.take(ROW)
    states[core, x] = back[my_slot]
    mine_at = back_at + core * NX + x
    for d in range(1, ROW):
        other, to = row_mate(d)
        slot = scan_slot(other, ROW, core)
        waits.append(send(back.at[slot], states.at[core, x], to, back_at + d, mine_at))

    g_both = pltpu.make_async_remote_copy(
        src_ref=g_peer, dst_ref=g_peer, send_sem=g_sem.at[1], recv_sem=g_sem.at[2],
        device_id=peer, device_id_type=MESH,
    )
    g_both.wait_recv()
    turned(g_peer, TOK)

    for d in range(1, ROW):
        other = lax.rem(j + ROW - d, ROW)
        c_of, x_of = lax.rem(other, 2), lax.div(other, 2)
        arrived(states.at[c_of, x_of], back_at + c_of * NX + x_of)
    start_state = states[0].reshape(INNER, STATE)
    end_grad = states[1].reshape(INNER, STATE)

    mix[...] = (loc_out[...] + lead[...] * dot(out_map, start_state, 1, 1)).astype(BF16)
    k = count.take()
    waits.append(send(mix, mix_peer, peer, k))
    mix_at = k

    grad_source = loc_src[...] + trail[...] * dot(in_map, end_grad, 1, 1)
    value = pre[...]
    gate = jax.nn.sigmoid(value)
    grad_value = grad_source * (gate * (1.0 + value * (1.0 - gate)))
    grad_pre[0:TOK, :] = grad_value
    k = count.take()
    halo_at = k
    waits.append(send(grad_pre.at[pl.ds(0, 8), :], grad_pre.at[pl.ds(TOK, 8), :], previous, k))
    terms = [
        jnp.sum(grad_value * ext[16 - tap : 16 - tap + TOK, :], axis=0, keepdims=True)
        for tap in range(TAPS)
    ]
    w_row[j] = jnp.concatenate(terms + [jnp.zeros((8 - TAPS, INNER), F32)], axis=0)
    w_at = count.take(ROW)
    for d in range(1, ROW):
        other, to = row_mate(d)
        waits.append(send(w_row.at[j], w_row.at[j], to, w_at + d, w_at + j))

    arrived(mix_peer, mix_at)

    axes = (at_x, at_y)
    far_at = [count.take(4) for _ in range(2)]
    one_at = [count.take(4) for _ in range(2)]
    three_at = [count.take(4) for _ in range(2)]
    both = jnp.concatenate([mix[...], mix_peer[...]], axis=0)

    def step_to(color, d):
        return axes[color](d)

    def handle(color, d, e, part):
        if d == 0:
            acc0[color, e] = part
        elif d == 2:
            send2[color, e] = part.astype(BF16)
            to = step_to(color, 1 if e < 2 else 3)
            waits.append(send(send2.at[color, e], relay.at[color, e], to, far_at[color] + e))
        elif d == 1 and e >= 2:
            send1[color, e] = part.astype(BF16)
            waits.append(send(send1.at[color, e], from_m.at[color, e], step_to(color, 1), one_at[color] + e))
        elif d == 3 and e < 2:
            send3[color, e] = part.astype(BF16)
            waits.append(send(send3.at[color, e], from_p.at[color, e], step_to(color, 3), three_at[color] + e))
        elif d == 1:
            hold1[color, e] = part
        else:
            hold3[color, e - 2] = part

    for dx, dy in ORDER:
        block = gt[lax.rem(x + dx, NX), lax.rem(y + dy, NY)]
        part = dot(block, both, 1, 0)
        handle(0, dx, dy, part[:, :128])
        handle(1, dy, dx, part[:, 128:])

    for e in (0, 1, 2, 3):
        for color in range(2):
            arrived(relay.at[color, e], far_at[color] + e)
            got = relay[color, e].astype(F32)
            if e < 2:
                send1[color, e] = (hold1[color, e] + got).astype(BF16)
                waits.append(send(send1.at[color, e], from_m.at[color, e], step_to(color, 1), one_at[color] + e))
            else:
                send3[color, e] = (hold3[color, e - 2] + got).astype(BF16)
                waits.append(send(send3.at[color, e], from_p.at[color, e], step_to(color, 3), three_at[color] + e))

    out_b[0] = (loc_b[...] + dot(ws[...], end_grad, 1, 0)).astype(BF16)
    out_c[0] = (loc_c[...] + dot(wg[...], start_state, 1, 0)).astype(BF16)
    arrived(grad_pre.at[pl.ds(TOK, 8), :], halo_at)
    last = jnp.where(s < NZ * ROW - 1, 1.0, 0.0)
    grad_pre[TOK : TOK + 8, :] = grad_pre[TOK : TOK + 8, :] * last
    value = jnp.zeros((TOK, INNER), F32)
    for tap in range(TAPS):
        value = value + taps_ref[tap : tap + 1, :] * grad_pre[tap : tap + TOK, :]
    out_x[0] = value.astype(BF16)

    wy_at = count.take(NY)
    for d in range(1, ROW):
        other = lax.rem(j + ROW - d, ROW)
        arrived(w_row.at[other], w_at + other)
    total = w_row[0]
    for q in range(1, ROW):
        total = total + w_row[q]
    w_y[y] = total
    for d in range(1, NY):
        waits.append(send(w_y.at[y], w_y.at[y], at_y(d), wy_at + d, wy_at + y))

    second_at = [count.take(4) for _ in range(2)]
    for e in (2, 1, 3, 0):
        for color in range(2):
            arrived(from_m.at[color, e], one_at[color] + e)
            arrived(from_p.at[color, e], three_at[color] + e)
            part = acc0[color, e] + from_m[color, e].astype(F32) + from_p[color, e].astype(F32)
            if e == 0:
                acc1[color] = part
            else:
                send_b[color, e] = part.astype(BF16)
                waits.append(
                    send(send_b.at[color, e], recv_b.at[color, e], axes[1 - color](e), second_at[color] + e)
                )

    wz_at = count.take(NZ)
    for d in range(1, NY):
        other = lax.rem(y + NY - d, NY)
        arrived(w_y.at[other], wy_at + other)
    total = w_y[0]
    for q in range(1, NY):
        total = total + w_y[q]
    w_z[z] = total
    for d in range(1, NZ):
        other, to = at_z(d)
        waits.append(send(w_z.at[z], w_z.at[z], to, wz_at + d, wz_at + z))

    for color in range(2):
        part = acc1[color]
        for e in range(1, 4):
            arrived(recv_b.at[color, e], second_at[color] + e)
            part = part + recv_b[color, e].astype(F32)
        for q in range(NZ):
            part3[q, :, color * 128 : (color + 1) * 128] = part[q * 32 : (q + 1) * 32]
            send_z[q, :, color * 128 : (color + 1) * 128] = part[q * 32 : (q + 1) * 32].astype(BF16)
    third_at = count.take(NZ)
    for d in range(1, NZ):
        other, to = at_z(d)
        waits.append(send(send_z.at[other], recv_z.at[d], to, third_at + d))

    for d in range(1, NZ):
        other = lax.rem(z + NZ - d, NZ)
        arrived(w_z.at[other], wz_at + other)
    total = w_z[0]
    for q in range(1, NZ):
        total = total + w_z[q]
    out_w[...] = total[0:TAPS] * SCALE

    final = part3[z]
    for d in range(1, NZ):
        arrived(recv_z.at[d], third_at + d)
        final = final + recv_z[d].astype(F32)
    out_p[...] = final

    g_both.wait_send()
    for later, pair_of in z_copies:

        @pl.when(later)
        def _(pair_of=pair_of):
            for copy in pair_of:
                copy.wait_send()

    for copy in waits:
        copy.wait_send()


SEMAPHORES = 192


def on_device(conv_input, in_map, out_map, step_size, decay_rate, skip_gain, conv_weight, grad_mixer, grad_output):
    vmem = pl.BlockSpec(memory_space=pltpu.VMEM)
    smem = pl.BlockSpec(memory_space=pltpu.SMEM)
    piece = (HEAD_DIM, STATE)
    half = (TOK, 128)
    scratch = [
        ((16, INNER), BF16), ((16 + TOK, INNER), F32), ((TOK, INNER), F32), ((TOK, INNER), BF16),
        ((TOK, INNER), BF16), ((TOK, INNER), BF16), ((TOK, INNER), F32), ((TOK, INNER), F32),
        ((8, 128), F32), ((2, HEADS, *piece), BF16), ((ROW, *piece), BF16), ((ROW, 8, 128), F32),
        ((ROW, *piece), F32), (piece, BF16), ((8, 128), F32), ((NZ, *piece), BF16), ((NZ, 8, 128), F32),
        (piece, F32), ((ROW, *piece), BF16), ((2, HEADS, *piece), BF16),
        ((TOK, INNER), F32), ((TOK, INNER), F32), ((TOK, STATE), F32), ((TOK, STATE), F32),
        ((TOK, INNER), BF16), ((TOK, INNER), BF16),
        ((NZ * NX, TOK, 128), BF16), ((NZ * NX, TOK, 128), BF16), ((NX, NY, TOK, 2 * TOK), BF16),
        ((2, 4, *half), F32), ((2, 2, *half), F32), ((2, 2, *half), F32), ((2, 4, *half), BF16),
        ((2, 4, *half), BF16), ((2, 4, *half), BF16), ((2, 4, *half), BF16), ((2, 4, *half), BF16),
        ((2, 4, *half), BF16), ((2, *half), F32), ((2, 4, *half), BF16), ((2, 4, *half), BF16),
        ((NZ, 32, INNER), F32), ((NZ, 32, INNER), BF16), ((NZ, 32, INNER), BF16),
        ((TOK + 8, INNER), F32), ((ROW, 8, INNER), F32), ((NY, 8, INNER), F32), ((NZ, 8, INNER), F32),
    ]
    return pl.pallas_call(
        kernel,
        name="mixer_backward",
        out_shape=(
            jax.ShapeDtypeStruct((1, TOK, INNER), BF16),
            jax.ShapeDtypeStruct((1, TOK, STATE), BF16),
            jax.ShapeDtypeStruct((1, TOK, STATE), BF16),
            jax.ShapeDtypeStruct((TAPS, INNER), F32),
            jax.ShapeDtypeStruct((32, INNER), F32),
        ),
        in_specs=[vmem, vmem, vmem, vmem, smem, smem, vmem, vmem, pl.BlockSpec(memory_space=pl.ANY)],
        out_specs=(vmem,) * 5,
        scratch_shapes=[
            *(pltpu.VMEM(shape, kind) for shape, kind in scratch),
            pltpu.SemaphoreType.DMA((3,)),
            pltpu.SemaphoreType.DMA((SEMAPHORES,)),
            pltpu.SemaphoreType.DMA((SEMAPHORES,)),
        ],
        compiler_params=pltpu.CompilerParams(
            collective_id=0, has_side_effects=True, vmem_limit_bytes=48 * 1024 * 1024
        ),
    )(conv_input, in_map, out_map, step_size[0].T, decay_rate, skip_gain, conv_weight, grad_mixer, grad_output)


def solution(mesh):
    split = P("dp", "seq", None)
    return jax.shard_map(
        on_device,
        mesh=mesh,
        in_specs=(split, split, split, split, P(), P(), P(), split, split),
        out_specs=(split, split, split, P(), P(("seq", "dp"), None)),
        check_vma=False,
    )
```

time: 342 us -> 66.6 us (0.19)
  waiting for transfers between devices: 181 us -> 0 us
  Pallas kernels: 0 us -> 53.8 us
  matrix products: 42.1 us -> 0 us
  blocking collectives: 39.6 us -> 0 us
  local copies, waits for them, and re-layouts: 36.5 us -> 11.5 us
  starting transfers between devices: 17 us -> 0 us
  between operations: 14 us -> 0.66 us
  other arithmetic: 10.6 us -> 0 us
    reduce_scatter x4 -> x0, waiting for transfers between devices: 94.9 us -> none  [reduced_to_own(): pieces = lax.psum_scatter(pieces, axes[k], scatter_dimension=0, tiled=True)]
    all_gather x1 -> x0, waiting for transfers between devices: 79.1 us -> none  [side_by_side(): lax.all_gather(both, axis, axis=dim, tiled=True)]
    pallas_call x0 -> x1, Pallas kernels: none -> 53.8 us  [on_device(): pl.pallas_call(kernel, name='mixer_backward', out_shape=(jax.ShapeDtypeSt...]
    dot_general x46 -> x0, matrix products: 42.1 us -> none  [the longest x1 8.82 us: on_device(): jnp.einsum('kh,khpn->hpn', backward_weight, pieces[1], precision=highest)]
    psum x4 -> x0, blocking collectives: 39.6 us -> none  [one_axis_at_a_time(): return functools.reduce(lax.psum, axes, value)]
    all_to_all x1 -> x0, starting transfers between devices: 12.9 us -> none  [copy_for_each(): lax.all_to_all(jnp.broadcast_to(value[None], (size, *value.shape)), axis,...]
    dot_general x1 -> x0, local copies, waits for them, and re-layouts: 9 us -> none  [on_device(): lax.dot_general(local_grad, mixer_out, (((0,), (0,)), ((), ())), preferre...]
    unnamed x10 -> x23, local copies, waits for them, and re-layouts: 2.79 us -> 11.5 us
  transfers between devices with their start and end apart: 8 -> 0, of which waited for: 5 -> 0; matrix products, arithmetic and copies ran while one was open for 4% -> 0% of each run, Pallas kernels for 0% -> 0%
where the time goes in v1:
time: 66.6 us; the launch traced here: 66 us
  Pallas kernels  53.8 us (81%)
  local copies, waits for them, and re-layouts  11.5 us (17%)
    pallas_call x1, Pallas kernels, on_device(): pl.pallas_call(kernel, name='mixer_backward', out_shape=(jax.ShapeDtypeSt...  53.8 us
    unnamed x23, local copies, waits for them, and re-layouts  11.5 us

profile of v1, /device:TPU:2, one launch (start us, length us, event | category | flops | bytes accessed | tf_op | source)
XLA Modules:
  0.0 66.0 jit_solution(6277256881653077074)
XLA Ops:
  0.6 0.0 copy-start
  0.6 2.2 %copy-done = bf16[1,256,8192]{2,1,0:T(8,128)(2,1)S(1)} copy-done((bf16[1,256,8192]{2,1,0:T(8,128)(2,1)S(1)}, bf16[1,256,8192]{2,1,0:T(8,128)(2,1)}, u32[]{:S(2)}) %copy-start) | copy-done | bytes 4194328
  2.8 0.0 copy-start.1
  2.8 0.9 %copy-done.1 = bf16[1,256,256]{2,1,0:T(8,128)(2,1)S(1)} copy-done((bf16[1,256,256]{2,1,0:T(8,128)(2,1)S(1)}, bf16[1,256,256]{2,1,0:T(8,128)(2,1)}, u32[]{:S(2)}) %copy-start.1) | copy-done | bytes 131096
  3.7 0.0 copy-start.2
  3.7 0.9 %copy-done.2 = bf16[1,256,256]{2,1,0:T(8,128)(2,1)S(1)} copy-done((bf16[1,256,256]{2,1,0:T(8,128)(2,1)S(1)}, bf16[1,256,256]{2,1,0:T(8,128)(2,1)}, u32[]{:S(2)}) %copy-start.2) | copy-done | bytes 131096
  4.6 0.0 copy-start.3
  4.6 0.8 %copy-done.3 = bf16[1,256,128]{2,1,0:T(8,128)(2,1)S(1)} copy-done((bf16[1,256,128]{2,1,0:T(8,128)(2,1)S(1)}, bf16[1,256,128]{2,1,0:T(8,128)(2,1)}, u32[]{:S(2)}) %copy-start.3) | copy-done | bytes 65560
  5.5 0.0 copy-start.4
  5.5 0.8 %copy-done.4 = bf16[1,256,128]{2,1,0:T(8,128)(2,1)S(1)} copy-done((bf16[1,256,128]{2,1,0:T(8,128)(2,1)S(1)}, bf16[1,256,128]{2,1,0:T(8,128)(2,1)}, u32[]{:S(2)}) %copy-start.4) | copy-done | bytes 65560
  6.3 0.0 copy-start.5
  6.3 0.7 %copy-done.5 = f32[1,256,4]{1,2,0:T(4,128)S(1)} copy-done((f32[1,256,4]{1,2,0:T(4,128)S(1)}, f32[1,256,4]{1,2,0:T(4,128)}, u32[]{:S(2)}) %copy-start.5) | copy-done | bytes 4120
  7.0 0.0 copy-start.6
  7.0 0.7 %copy-done.6 = f32[4,256]{1,0:T(4,128)S(1)} copy-done((f32[4,256]{1,0:T(4,128)S(1)}, f32[4,256]{1,0:T(4,128)}, u32[]{:S(2)}) %copy-start.6) | copy-done | bytes 4120
  7.7 0.0 copy-start.7
  7.7 0.7 copy-done.7
  8.3 0.0 copy-start.8
  8.3 0.7 copy-done.8
  9.0 53.8 %mixer_backward.1 = (bf16[1,256,256]{2,1,0:T(8,128)(2,1)S(1)}, bf16[1,256,128]{2,1,0:T(8,128)(2,1)S(1)}, bf16[1,256,128]{2,1,0:T(8,128)(2,1)S(1)}, f32[4,256]{1,0:T(4,128)S(1)}, f32[32,256]{1,0:T(8,128)S(1)}) custom-call(bf16[1,256,256]{2,1,0:T(8,128)(2,1)S(1)} %copy-done.1, bf16[1,256,128]{2,1,0:T(8,128)(2,1)S(1)} %copy-done.3, ...), custom_call_target="tpu_custom_call" | custom-call | tf_op jit(solution)/shard_map/mixer_backward/pallas_call | solution.py:497
  62.8 0.7 copy.19
  63.5 0.6 copy.20
  64.1 0.6 copy.21
  64.7 0.6 copy.22
  65.3 0.6 copy.23
Async XLA Ops:
  0.6 2.2 %copy-start = (bf16[1,256,8192]{2,1,0:T(8,128)(2,1)S(1)}, bf16[1,256,8192]{2,1,0:T(8,128)(2,1)}, u32[]{:S(2)}) copy-start(bf16[1,256,8192]{2,1,0:T(8,128)(2,1)} %g_ref.1) | copy-start | bytes 12582916
  2.8 0.9 %copy-start.1 = (bf16[1,256,256]{2,1,0:T(8,128)(2,1)S(1)}, bf16[1,256,256]{2,1,0:T(8,128)(2,1)}, u32[]{:S(2)}) copy-start(bf16[1,256,256]{2,1,0:T(8,128)(2,1)} %x_ref.1) | copy-start | bytes 393220
  3.7 0.9 %copy-start.2 = (bf16[1,256,256]{2,1,0:T(8,128)(2,1)S(1)}, bf16[1,256,256]{2,1,0:T(8,128)(2,1)}, u32[]{:S(2)}) copy-start(bf16[1,256,256]{2,1,0:T(8,128)(2,1)} %up_ref.1) | copy-start | bytes 393220
  4.6 0.8 %copy-start.3 = (bf16[1,256,128]{2,1,0:T(8,128)(2,1)S(1)}, bf16[1,256,128]{2,1,0:T(8,128)(2,1)}, u32[]{:S(2)}) copy-start(bf16[1,256,128]{2,1,0:T(8,128)(2,1)} %b_ref.1) | copy-start | bytes 196612
  5.5 0.8 %copy-start.4 = (bf16[1,256,128]{2,1,0:T(8,128)(2,1)S(1)}, bf16[1,256,128]{2,1,0:T(8,128)(2,1)}, u32[]{:S(2)}) copy-start(bf16[1,256,128]{2,1,0:T(8,128)(2,1)} %c_ref.1) | copy-start | bytes 196612
  6.3 0.7 %copy-start.5 = (f32[1,256,4]{1,2,0:T(4,128)S(1)}, f32[1,256,4]{1,2,0:T(4,128)}, u32[]{:S(2)}) copy-start(f32[1,256,4]{1,2,0:T(4,128)} %param.12) | copy-start | bytes 12292
  7.0 0.7 %copy-start.6 = (f32[4,256]{1,0:T(4,128)S(1)}, f32[4,256]{1,0:T(4,128)}, u32[]{:S(2)}) copy-start(f32[4,256]{1,0:T(4,128)} %taps_ref.1) | copy-start | bytes 12292
  7.7 0.7 copy-start.7
  8.3 0.7 copy-start.8

commit v2 on v1

v2 whole, which is shorter than its diff:
```python
import contextlib

import jax
import jax.numpy as jnp
from jax import lax
from jax.experimental import pallas as pl
from jax.experimental.pallas import tpu as pltpu
from jax.sharding import PartitionSpec as P

MESH = pl.DeviceIdType.MESH
F32 = jnp.float32
BF16 = jnp.bfloat16

NZ, NX, NC, NY = 8, 4, 2, 4
ROW = NX * NC
HEADS, HEAD_DIM, STATE = 4, 64, 128
TOK, INNER, TAPS = 256, 256, 4
EARLY = 6
SCALE = float(TOK * NZ * NX * NC * NY) ** -0.5
ORDER = (
    (2, 2), (2, 1), (1, 2), (2, 0), (0, 2), (2, 3), (3, 2), (1, 1),
    (1, 3), (3, 1), (3, 0), (0, 3), (0, 1), (1, 0), (3, 3), (0, 0),
)
PLUS, MINUS = (2, 0), (1, 3)
EARLY = 6
SCALE = float(TOK * NZ * NX * NC * NY) ** -0.5
ORDER = (
    (2, 0), (0, 2), (2, 1), (1, 2), (2, 2), (2, 3), (3, 2), (1, 3),
    (3, 1), (3, 0), (0, 3), (1, 0), (0, 1), (1, 1), (3, 3), (0, 0),
)


class Phases:
    def __init__(self):
        self.open = contextlib.ExitStack()

    def __call__(self, name):
        self.open.close()
        self.open.enter_context(jax.named_scope(name))


class Counter:
    def __init__(self):
        self.used = 0

    def take(self, count=1):
        first = self.used
        self.used += count
        return first


def dot(a, b, da, db):
    return lax.dot_general(a, b, (((da,), (db,)), ((), ())), preferred_element_type=F32)


def exact(a, b, da, db):
    return lax.dot_general(
        a,
        b,
        (((da,), (db,)), ((), ())),
        precision=lax.Precision.HIGHEST,
        preferred_element_type=F32,
    )


def scan_slot(place, size, core):
    return place + core * (size - 1 - 2 * place)


def kernel(
    x_hbm, b_hbm, c_hbm, step_hbm, rate_hbm, skip_hbm, taps_hbm, up_hbm, g_ref,
    x_out, b_out, c_out, w_out, p_out,
    out_x, out_b, out_c, out_w, out_p,
    x_ref, b_ref, c_ref, step_ref, taps_ref, up_ref, rate_ref, skip_ref,
    halo, ext, pre, src, ws, wg, lead, trail,
    tot, pieces, row_p, row_t, prefix, row_sum, row_log, z_p, z_t, z_state, back, states,
    begun, loc_out, loc_src, loc_b, loc_c, mix, mix_peer,
    g_own, g_peer, gt,
    acc0, hold1, hold3, send2, relay, send1, send3, from_m, from_p, acc1, send_b, recv_b,
    part3, send_z, recv_z, grad_pre, w_row, w_y, w_z,
    in_sem, out_sem, g_sem, ssem, rsem,
):
    phase = Phases()
    phase("entry")
    inputs = [
        pltpu.make_async_copy(source, target, in_sem.at[i])
        for i, (source, target) in enumerate(
            (
                (step_hbm, step_ref), (rate_hbm, rate_ref), (skip_hbm, skip_ref), (up_hbm.at[0], up_ref),
                (b_hbm.at[0], b_ref), (c_hbm.at[0], c_ref), (x_hbm.at[0], x_ref), (taps_hbm, taps_ref),
            )
        )
    ]
    outputs = [
        pltpu.make_async_copy(source, target, out_sem.at[i])
        for i, (source, target) in enumerate(
            (
                (out_x, x_out.at[0]), (out_b, b_out.at[0]), (out_c, c_out.at[0]),
                (out_w, w_out), (out_p, p_out),
            )
        )
    ]
    for copy in inputs:
        copy.start()
    s = lax.axis_index("seq")
    y = lax.axis_index("dp")
    core = lax.rem(s, 2)
    x = lax.rem(lax.div(s, 2), 4)
    z = lax.div(s, ROW)
    j = lax.rem(s, ROW)
    sends, count = Counter(), Counter()
    sent = []

    def remote(source, target, to, index, slot):
        return pltpu.make_async_remote_copy(
            src_ref=source,
            dst_ref=target,
            send_sem=ssem.at[index],
            recv_sem=rsem.at[slot],
            device_id=to,
            device_id_type=MESH,
        )

    def send(source, target, to, index, slot):
        remote(source, target, to, index, slot).start()

    def arrived(target, slot):
        remote(target, target, (s, y), 0, slot).wait_recv()

    def group(whole):
        index = sends.take()
        sent.append((whole, index))
        return index

    def row_mate(d):
        other = lax.rem(j + d, ROW)
        return other, (z * ROW + other, y)

    def at_x(d):
        return ((z * NX + lax.rem(x + d, NX)) * NC + core, y)

    def at_y(d):
        return (s, lax.rem(y + d, NY))

    def at_z(d):
        other = lax.rem(z + d, NZ)
        return other, (other * ROW + j, y)

    peer = (s + 1 - 2 * core, y)
    following = (lax.rem(s + 1, NZ * ROW), y)
    previous = (lax.rem(s + NZ * ROW - 1, NZ * ROW), y)

    barrier = pltpu.get_barrier_semaphore()
    partners = [row_mate(d)[1] for d in range(1, ROW)]
    partners += [at_z(d)[1] for d in range(1, NZ)]
    partners += [at_y(d) for d in range(1, NY)]
    partners += [following, previous]
    for partner in partners:
        pl.semaphore_signal(barrier, inc=1, device_id=partner, device_id_type=MESH)

    @pl.loop(0, NZ * NX)
    def _(i):
        at = pl.multiple_of((i * NC + core) * 128, 128)
        pltpu.make_async_copy(g_ref.at[0, :, pl.ds(at, 128)], g_own.at[i], g_sem.at[0]).start()

    phase("inputs")
    for copy in inputs:
        copy.wait()

    phase("decays")
    steps = step_ref[...]
    head_row = lax.broadcasted_iota(jnp.int32, (HEADS, TOK), 0)
    rates = jnp.full((HEADS, TOK), rate_ref[0], F32)
    for h in range(1, HEADS):
        rates = jnp.where(head_row == h, rate_ref[h], rates)
    token_r = lax.broadcasted_iota(jnp.int32, (TOK, TOK), 0)
    token_c = lax.broadcasted_iota(jnp.int32, (TOK, TOK), 1)
    upper = jnp.where(token_r <= token_c, 1.0, 0.0).astype(F32)
    sums = exact(-steps * rates, upper, 1, 0)
    rows = jnp.concatenate([sums, steps], axis=0)
    cols = rows.T
    head_of = lax.div(lax.broadcasted_iota(jnp.int32, (8, INNER), 1), HEAD_DIM)
    row_of = lax.broadcasted_iota(jnp.int32, (8, INNER), 0)
    sums_wide = exact(rows, jnp.where(row_of == head_of, 1.0, 0.0).astype(F32), 0, 0)
    step_wide = exact(rows, jnp.where(row_of == head_of + HEADS, 1.0, 0.0).astype(F32), 0, 0)
    lead[...] = jnp.exp(sums_wide)
    trail[...] = step_wide * jnp.exp(sums_wide[TOK - 1 : TOK, :] - sums_wide)
    tot[...] = jnp.broadcast_to(rows[:, TOK - 1 : TOK], (8, 128))
    upstream = up_ref[...]
    in_map = b_ref[...]
    out_map = c_ref[...]
    wg[...] = (upstream.astype(F32) * lead[...]).astype(BF16)
    grad_piece = dot(wg[...], out_map, 0, 0).astype(BF16)
    for h in range(HEADS):
        pieces[1, h] = grad_piece[h * HEAD_DIM : (h + 1) * HEAD_DIM]
    ext[0:16, :] = jnp.zeros((16, INNER), F32)
    ext[16:, :] = x_ref[...].astype(F32)

    phase("barrier")
    pl.semaphore_wait(barrier, len(partners))

    phase("sends")
    halo_at = count.take()
    halo_out = remote(x_ref.at[pl.ds(TOK - 16, 16), :], halo, following, sends.take(), halo_at)
    not_last, not_first = s < NZ * ROW - 1, s > 0

    @pl.when(not_last)
    def _():
        halo_out.start()

    slot_j = [scan_slot(j, ROW, c) for c in range(NC)]
    my_slot = scan_slot(j, ROW, core)
    total_at = count.take()
    total_out = group(row_t.at[pl.ds(0, ROW - 1)])
    row_t[my_slot] = tot[...]
    for d in range(1, ROW):
        other, to = row_mate(d)
        send(tot, row_t.at[scan_slot(j, ROW, lax.rem(other, 2))], to, total_out, total_at)

    piece_at = count.take()
    piece_out = group(row_p.at[pl.ds(0, ROW - 1)])

    def pieces_to(direction):
        @pl.when(core == direction)
        def _():
            row_p[my_slot] = pieces[direction, x]

        for d in range(NX):
            to_x = lax.rem(x + d, NX)
            copy = remote(
                pieces.at[direction, to_x],
                row_p.at[slot_j[direction]],
                ((z * NX + to_x) * NC + direction, y),
                piece_out,
                piece_at,
            )
            if d == 0:

                @pl.when(core != direction)
                def _():
                    copy.start()
            else:
                copy.start()

    guarded = [(not_last, [halo_out])]
    pieces_to(1)

    phase("conv")
    value = jnp.zeros((TOK, INNER), F32)
    for tap in range(TAPS):
        value = value + taps_ref[tap : tap + 1, :] * ext[16 - tap : 16 - tap + TOK, :]
    pre[...] = value

    phase("halo_wait")

    @pl.when(not_first)
    def _():
        arrived(halo, halo_at)
        ext[0:16, :] = halo[...].astype(F32)

    value = jnp.zeros((8, INNER), F32)
    for tap in range(TAPS):
        value = value + taps_ref[tap : tap + 1, :] * ext[16 - tap : 24 - tap, :]
    pre[0:8, :] = value

    phase("source")
    value = pre[...]
    source = (value * jax.nn.sigmoid(value)).astype(BF16)
    src[...] = source
    ws[...] = (source.astype(F32) * trail[...]).astype(BF16)
    state_piece = dot(ws[...], in_map, 0, 0).astype(BF16)
    for h in range(HEADS):
        pieces[0, h] = state_piece[h * HEAD_DIM : (h + 1) * HEAD_DIM]
    pieces_to(0)

    @pl.loop(0, NZ * NX)
    def _(i):
        at = pl.multiple_of((i * NC + 1 - core) * 128, 128)
        pltpu.make_async_remote_copy(
            src_ref=g_ref.at[0, :, pl.ds(at, 128)],
            dst_ref=g_peer.at[i],
            send_sem=g_sem.at[1],
            recv_sem=g_sem.at[2],
            device_id=peer,
            device_id_type=MESH,
        ).start()

    phase("inside")
    scores = dot(out_map, in_map, 1, 1)
    causal = token_r >= token_c
    low = lax.broadcasted_iota(jnp.int32, (TOK, 128), 1) < HEAD_DIM
    for pair in range(HEADS // 2):
        lanes = slice(pair * 128, (pair + 1) * 128)
        sp = src[:, lanes]
        upp = up_ref[:, lanes]
        outs, grads = [], []
        for half in range(2):
            h = 2 * pair + half
            mine = low if half == 0 else jnp.logical_not(low)
            spread = cols[:, h : h + 1] - rows[h : h + 1, :]
            seg = jnp.where(causal, jnp.exp(jnp.where(causal, spread, 0.0)), 0.0)
            seg = seg * rows[HEADS + h : HEADS + h + 1, :]
            mixing = (seg * scores).astype(BF16)
            outs.append(dot(mixing, sp, 1, 0))
            grads.append(dot(mixing, upp, 0, 0))
            up_only = jnp.where(mine, upp.astype(F32), 0.0).astype(BF16)
            weighted = (seg * dot(up_only, sp, 1, 1)).astype(BF16)
            part_b = dot(weighted, out_map, 0, 0)
            part_c = dot(weighted, in_map, 1, 0)
            if h == 0:
                loc_b[...] = part_b
                loc_c[...] = part_c
            else:
                loc_b[...] += part_b
                loc_c[...] += part_c
        gain = jnp.where(low, skip_ref[2 * pair], skip_ref[2 * pair + 1])
        loc_out[:, lanes] = jnp.where(low, outs[0], outs[1]) + gain * sp.astype(F32)
        loc_src[:, lanes] = jnp.where(low, grads[0], grads[1]) + gain * upp.astype(F32)

    phase("row_wait")
    arrived(row_t.at[pl.ds(0, ROW - 1)], total_at)
    arrived(row_p.at[pl.ds(0, ROW - 1)], piece_at)
    phase("row_scan")
    running = jnp.zeros((HEAD_DIM, STATE), F32)
    decayed = jnp.zeros((1, 128), F32)
    before = []
    for q in range(ROW):
        prefix[q] = running
        before.append(decayed)
        own = row_t[q, pl.ds(x, 1), :]
        running = jnp.exp(own) * running + row_p[q].astype(F32)
        decayed = decayed + own
    row_sum[...] = running.astype(BF16)
    row_log[...] = jnp.broadcast_to(decayed, (8, 128))

    my_z = scan_slot(z, NZ, core)
    zs_at = count.take(NZ - 1)
    zl_at = count.take(NZ - 1)
    for d in range(1, NZ):
        other, to = at_z(d)
        later = scan_slot(other, NZ, core) > my_z
        pair_of = [
            remote(source, target.at[my_z], to, sends.take(), base + my_z)
            for source, target, base in ((row_log, z_t, zl_at), (row_sum, z_p, zs_at))
        ]
        guarded.append((later, pair_of))

        @pl.when(later)
        def _(pair_of=pair_of):
            for copy in pair_of:
                copy.start()

    def turned(held, column):
        @pl.loop(0, NZ * NX)
        def _(i):
            xi = lax.rem(i, NX)
            zi = pl.multiple_of(lax.div(i, NX) * 32, 32)
            block = held[i].T
            for yi in range(NY):
                gt[xi, yi, pl.ds(zi, 32), column : column + TOK] = block[yi * 32 : (yi + 1) * 32]

    phase("turn_own")
    pltpu.make_async_copy(g_own, g_own, g_sem.at[0]).wait()
    turned(g_own, 0)

    phase("z_wait_scan")
    z_state[...] = jnp.zeros_like(z_state)
    for q in range(NZ - 1):

        @pl.when(q < my_z)
        def _(q=q):
            arrived(z_t.at[q], zl_at + q)
            arrived(z_p.at[q], zs_at + q)
            z_state[...] = jnp.exp(z_t[q, 0:1, :]) * z_state[...] + z_p[q].astype(F32)

    entering = z_state[...]
    for q in range(ROW):
        back[q] = (jnp.exp(before[q]) * entering + prefix[q]).astype(BF16)
    back_at = count.take()
    back_out = group(row_p.at[pl.ds(0, ROW - 1)])
    states[core, x] = back[my_slot]
    for d in range(1, ROW):
        other, to = row_mate(d)
        send(back.at[scan_slot(other, ROW, core)], states.at[core, x], to, back_out, back_at)

    g_both = pltpu.make_async_remote_copy(
        src_ref=g_peer, dst_ref=g_peer, send_sem=g_sem.at[1], recv_sem=g_sem.at[2],
        device_id=peer, device_id_type=MESH,
    )
    phase("turn_peer")
    g_both.wait_recv()
    turned(g_peer, TOK)

    phase("states_wait")
    arrived(row_p.at[pl.ds(0, ROW - 1)], back_at)
    start_state = states[0].reshape(INNER, STATE)
    end_grad = states[1].reshape(INNER, STATE)

    phase("mix")
    mix[...] = (loc_out[...] + lead[...] * dot(out_map, start_state, 1, 1)).astype(BF16)
    mix_at = count.take()
    send(mix, mix_peer, peer, group(mix), mix_at)

    phase("grad_pre")
    grad_source = loc_src[...] + trail[...] * dot(in_map, end_grad, 1, 1)
    value = pre[...]
    gate = jax.nn.sigmoid(value)
    grad_value = grad_source * (gate * (1.0 + value * (1.0 - gate)))
    grad_pre[0:TOK, :] = grad_value
    tail_at = count.take()
    tail_out = remote(
        grad_pre.at[pl.ds(0, 8), :], grad_pre.at[pl.ds(TOK, 8), :], previous, sends.take(), tail_at
    )
    guarded.append((not_first, [tail_out]))

    @pl.when(not_first)
    def _():
        tail_out.start()

    @pl.when(jnp.logical_not(not_last))
    def _():
        grad_pre[TOK : TOK + 8, :] = jnp.zeros((8, INNER), F32)

    terms = [
        jnp.sum(grad_value * ext[16 - tap : 16 - tap + TOK, :], axis=0, keepdims=True)
        for tap in range(TAPS)
    ]
    w_row[j] = jnp.concatenate(terms + [jnp.zeros((8 - TAPS, INNER), F32)], axis=0)
    w_at = count.take()
    w_out_at = group(w_row.at[pl.ds(0, ROW - 1)])
    for d in range(1, ROW):
        send(w_row.at[j], w_row.at[j], row_mate(d)[1], w_out_at, w_at)

    axes = (at_x, at_y)
    far_at = [count.take(4) for _ in range(2)]
    one_at = [count.take(4) for _ in range(2)]
    three_at = [count.take(4) for _ in range(2)]
    far_out, one_out, three_out = group(send2), group(send1), group(send3)
    def step_to(color, d):
        return axes[color](d)

    def handle(color, d, e, part):
        if d == 0:
            acc0[color, e] = part
        elif d == 2:
            send2[color, e] = part.astype(BF16)
            to = step_to(color, 1 if e in PLUS else 3)
            send(send2.at[color, e], relay.at[color, e], to, far_out, far_at[color] + e)
        elif d == 1 and e not in PLUS:
            send1[color, e] = part.astype(BF16)
            send(send1.at[color, e], from_m.at[color, e], step_to(color, 1), one_out, one_at[color] + e)
        elif d == 3 and e in PLUS:
            send3[color, e] = part.astype(BF16)
            send(send3.at[color, e], from_p.at[color, e], step_to(color, 3), three_out, three_at[color] + e)
        elif d == 1:
            hold1[color, PLUS.index(e)] = part
        else:
            hold3[color, MINUS.index(e)] = part

    def rows_of(dx, dy, column):
        return gt[lax.rem(x + dx, NX), lax.rem(y + dy, NY), :, column : column + TOK]

    phase("project_own")
    for i, (dx, dy) in enumerate(ORDER[:EARLY]):
        begun[i] = dot(rows_of(dx, dy, 0), mix[...], 1, 0)
    phase("mix_wait")
    arrived(mix_peer, mix_at)
    phase("project")
    for i, (dx, dy) in enumerate(ORDER):
        part = begun[i] if i < EARLY else dot(rows_of(dx, dy, 0), mix[...], 1, 0)
        part = part + dot(rows_of(dx, dy, TOK), mix_peer[...], 1, 0)
        handle(0, dx, dy, part[:, :128])
        handle(1, dy, dx, part[:, 128:])

    phase("relay")
    for e in (2, 1, 0, 3):
        for color in range(2):
            arrived(relay.at[color, e], far_at[color] + e)
            got = relay[color, e].astype(F32)
            if e in PLUS:
                send1[color, e] = (hold1[color, PLUS.index(e)] + got).astype(BF16)
                send(send1.at[color, e], from_m.at[color, e], step_to(color, 1), one_out, one_at[color] + e)
            else:
                send3[color, e] = (hold3[color, MINUS.index(e)] + got).astype(BF16)
                send(send3.at[color, e], from_p.at[color, e], step_to(color, 3), three_out, three_at[color] + e)

    phase("maps")
    out_b[...] = (loc_b[...] + dot(ws[...], end_grad, 1, 0)).astype(BF16)
    out_c[...] = (loc_c[...] + dot(wg[...], start_state, 1, 0)).astype(BF16)

    @pl.when(not_last)
    def _():
        arrived(grad_pre.at[pl.ds(TOK, 8), :], tail_at)

    value = jnp.zeros((TOK, INNER), F32)
    for tap in range(TAPS):
        value = value + taps_ref[tap : tap + 1, :] * grad_pre[tap : tap + TOK, :]
    out_x[...] = value.astype(BF16)
    for copy in outputs[:3]:
        copy.start()

    phase("taps_row")
    wy_at = count.take()
    wy_out = group(w_y.at[pl.ds(0, NY - 1)])
    arrived(w_row.at[pl.ds(0, ROW - 1)], w_at)
    total = w_row[0]
    for q in range(1, ROW):
        total = total + w_row[q]
    w_y[y] = total
    for d in range(1, NY):
        send(w_y.at[y], w_y.at[y], at_y(d), wy_out, wy_at)

    phase("stage1_wait")
    second_at = [count.take() for _ in range(2)]
    second_out = group(send_b.at[:, pl.ds(1, 3)])
    for e in (2, 1, 3, 0):
        for color in range(2):
            arrived(from_m.at[color, e], one_at[color] + e)
            arrived(from_p.at[color, e], three_at[color] + e)
            part = acc0[color, e] + from_m[color, e].astype(F32) + from_p[color, e].astype(F32)
            if e == 0:
                acc1[color] = part
            else:
                send_b[color, e] = part.astype(BF16)
                send(send_b.at[color, e], recv_b.at[color, e], axes[1 - color](e), second_out, second_at[color])

    phase("taps_y")
    wz_at = count.take()
    wz_out = group(w_z.at[pl.ds(0, NZ - 1)])
    arrived(w_y.at[pl.ds(0, NY - 1)], wy_at)
    total = w_y[0]
    for q in range(1, NY):
        total = total + w_y[q]
    w_z[z] = total
    for d in range(1, NZ):
        send(w_z.at[z], w_z.at[z], at_z(d)[1], wz_out, wz_at)

    phase("stage2_wait")
    for color in range(2):
        part = acc1[color]
        arrived(recv_b.at[color, pl.ds(1, 3)], second_at[color])
        for e in range(1, 4):
            part = part + recv_b[color, e].astype(F32)
        for q in range(NZ):
            part3[q, :, color * 128 : (color + 1) * 128] = part[q * 32 : (q + 1) * 32]
            send_z[q, :, color * 128 : (color + 1) * 128] = part[q * 32 : (q + 1) * 32].astype(BF16)
    third_at = count.take()
    third_out = group(send_z.at[pl.ds(0, NZ - 1)])
    for d in range(1, NZ):
        other, to = at_z(d)
        send(send_z.at[other], recv_z.at[d], to, third_out, third_at)

    phase("taps_z")
    arrived(w_z.at[pl.ds(0, NZ - 1)], wz_at)
    total = w_z[0]
    for q in range(1, NZ):
        total = total + w_z[q]
    out_w[...] = total[0:TAPS] * SCALE
    outputs[3].start()

    phase("stage3_wait")
    final = part3[z]
    arrived(recv_z.at[pl.ds(0, NZ - 1)], third_at)
    for d in range(1, NZ):
        final = final + recv_z[d].astype(F32)
    out_p[...] = final
    outputs[4].start()

    phase("drain")
    assert (sends.used, count.used) == (SENDS, ARRIVALS), (sends.used, count.used)
    g_both.wait_send()
    for later, pair_of in guarded:

        @pl.when(later)
        def _(pair_of=pair_of):
            for copy in pair_of:
                copy.wait_send()

    for whole, index in sent:
        remote(whole, whole, (s, y), index, 0).wait_send()
    for copy in outputs:
        copy.wait()
    phase.open.close()


def writer(*refs):
    n = (len(refs) - 2) // 3
    taken, given, held, sems = refs[:n], refs[n : 2 * n], refs[2 * n : 3 * n], refs[3 * n :]
    reads = [pltpu.make_async_copy(taken[i], held[i], sems[0].at[i]) for i in range(n)]
    writes = [pltpu.make_async_copy(held[i], given[i], sems[1].at[i]) for i in range(n)]
    for copy in reads:
        copy.start()
    for read, write in zip(reads, writes):
        read.wait()
        write.start()
    for copy in writes:
        copy.wait()


SENDS, ARRIVALS = 28, 50
VMEM_GRANT = 67043328


def on_device(conv_input, in_map, out_map, step_size, decay_rate, skip_gain, conv_weight, grad_mixer, grad_output):
    hbm = pl.BlockSpec(memory_space=pltpu.HBM)
    piece = (HEAD_DIM, STATE)
    half = (TOK, 128)
    scratch = [
        ((TOK, INNER), BF16), ((TOK, STATE), BF16), ((TOK, STATE), BF16), ((TAPS, INNER), F32), ((32, INNER), F32),
        ((TOK, INNER), BF16), ((TOK, STATE), BF16), ((TOK, STATE), BF16), ((HEADS, TOK), F32),
        ((TAPS, INNER), F32), ((TOK, INNER), BF16),
    ]
    scratch2 = [
        ((16, INNER), BF16), ((16 + TOK, INNER), F32), ((TOK, INNER), F32), ((TOK, INNER), BF16),
        ((TOK, INNER), BF16), ((TOK, INNER), BF16), ((TOK, INNER), F32), ((TOK, INNER), F32),
        ((8, 128), F32), ((2, HEADS, *piece), BF16), ((ROW, *piece), BF16), ((ROW, 8, 128), F32),
        ((ROW, *piece), F32), (piece, BF16), ((8, 128), F32), ((NZ, *piece), BF16), ((NZ, 8, 128), F32),
        (piece, F32), ((ROW, *piece), BF16), ((2, HEADS, *piece), BF16), ((EARLY, TOK, INNER), F32),
        ((TOK, INNER), F32), ((TOK, INNER), F32), ((TOK, STATE), F32), ((TOK, STATE), F32),
        ((TOK, INNER), BF16), ((TOK, INNER), BF16),
        ((NZ * NX, TOK, 128), BF16), ((NZ * NX, TOK, 128), BF16), ((NX, NY, TOK, 2 * TOK), BF16),
        ((2, 4, *half), F32), ((2, 2, *half), F32), ((2, 2, *half), F32), ((2, 4, *half), BF16),
        ((2, 4, *half), BF16), ((2, 4, *half), BF16), ((2, 4, *half), BF16), ((2, 4, *half), BF16),
        ((2, 4, *half), BF16), ((2, *half), F32), ((2, 4, *half), BF16), ((2, 4, *half), BF16),
        ((NZ, 32, INNER), F32), ((NZ, 32, INNER), BF16), ((NZ, 32, INNER), BF16),
        ((TOK + 8, INNER), F32), ((ROW, 8, INNER), F32), ((NY, 8, INNER), F32), ((NZ, 8, INNER), F32),
    ]
    outs = (
        jax.ShapeDtypeStruct((1, TOK, INNER), BF16),
        jax.ShapeDtypeStruct((1, TOK, STATE), BF16),
        jax.ShapeDtypeStruct((1, TOK, STATE), BF16),
        jax.ShapeDtypeStruct((TAPS, INNER), F32),
        jax.ShapeDtypeStruct((32, INNER), F32),
    )
    results = pl.pallas_call(
        kernel,
        name="mixer_backward",
        out_shape=outs,
        in_specs=[hbm] * 9,
        out_specs=(hbm,) * 5,
        scratch_shapes=[
            *(pltpu.VMEM(shape, kind) for shape, kind in scratch),
            pltpu.SMEM((HEADS,), F32),
            pltpu.SMEM((HEADS,), F32),
            *(pltpu.VMEM(shape, kind) for shape, kind in scratch2),
            pltpu.SemaphoreType.DMA((8,)),
            pltpu.SemaphoreType.DMA((5,)),
            pltpu.SemaphoreType.DMA((3,)),
            pltpu.SemaphoreType.DMA((SENDS,)),
            pltpu.SemaphoreType.DMA((ARRIVALS,)),
        ],
        compiler_params=pltpu.CompilerParams(
            collective_id=0, has_side_effects=True, vmem_limit_bytes=VMEM_GRANT
        ),
    )(conv_input, in_map, out_map, step_size[0].T, decay_rate, skip_gain, conv_weight, grad_mixer, grad_output)
    return pl.pallas_call(
        writer,
        name="writer",
        out_shape=outs,
        in_specs=[hbm] * 5,
        out_specs=(hbm,) * 5,
        scratch_shapes=[
            *(pltpu.VMEM(out.shape, out.dtype) for out in outs),
            pltpu.SemaphoreType.DMA((5,)),
            pltpu.SemaphoreType.DMA((5,)),
        ],
        compiler_params=pltpu.CompilerParams(vmem_limit_bytes=VMEM_GRANT),
    )(*results)


def solution(mesh):
    split = P("dp", "seq", None)
    return jax.shard_map(
        on_device,
        mesh=mesh,
        in_specs=(split, split, split, split, P(), P(), P(), split, split),
        out_specs=(split, split, split, P(), P(("seq", "dp"), None)),
        check_vma=False,
    )
```

time: 66.6 us -> 51.4 us (0.77)
  local copies, waits for them, and re-layouts: 11.5 us -> 0 us
  Pallas kernels: 53.8 us -> 50.3 us
    unnamed x23 -> x0, local copies, waits for them, and re-layouts: 11.5 us -> none
    pallas_call x1 -> x2, Pallas kernels: 53.8 us -> 50.3 us  [the longest x1 48.6 us: on_device(): pl.pallas_call(kernel, name='mixer_backward', out_shape=outs, in_specs=[h...]
where the time goes in v2:
time: 51.4 us; the launch traced here: 50.9 us
  Pallas kernels  50.3 us (98%)
  between operations  0.64 us (1%)
    pallas_call x1, Pallas kernels, on_device(): pl.pallas_call(kernel, name='mixer_backward', out_shape=outs, in_specs=[h...  48.6 us
    pallas_call x1, Pallas kernels, on_device(): pl.pallas_call(writer, name='writer', out_shape=outs, in_specs=[hbm] * 5,...  1.7 us

profile of v2, /device:TPU:2, one launch (start us, length us, event | category | flops | bytes accessed | tf_op | source)
XLA Modules:
  0.0 50.9 jit_solution(14435012618615694862)
XLA Ops:
  0.6 48.6 %mixer_backward.1 = (bf16[1,256,256]{2,1,0:T(8,128)(2,1)}, bf16[1,256,128]{2,1,0:T(8,128)(2,1)}, bf16[1,256,128]{2,1,0:T(8,128)(2,1)}, f32[4,256]{1,0:T(4,128)}, f32[32,256]{1,0:T(8,128)}) custom-call(bf16[1,256,256]{2,1,0:T(8,128)(2,1)} %x_hbm.1, bf16[1,256,128]{2,1,0:T(8,128)(2,1)} %b_hbm.1, bf16[1,256,128]{2,1,0:T(8,128)(2,1)} %c_hbm.1, ...), custom_call_target="tpu_custom_call" | custom-call | tf_op jit(solution)/shard_map/mixer_backward/pallas_call | solution.py:635
  49.2 1.7 %writer.1 = (bf16[1,256,256]{2,1,0:T(8,128)(2,1)}, bf16[1,256,128]{2,1,0:T(8,128)(2,1)}, bf16[1,256,128]{2,1,0:T(8,128)(2,1)}, f32[4,256]{1,0:T(4,128)}, f32[32,256]{1,0:T(8,128)}) custom-call(bf16[1,256,256]{2,1,0:T(8,128)(2,1)} %get-tuple-element.10.refs_0_, bf16[1,256,128]{2,1,0:T(8,128)(2,1)} %get-tuple-element.11.refs_1_, ...), custom_call_target="tpu_custom_call" | custom-call | tf_op jit(solution)/shard_map/writer/pallas_call | solution.py:656

commit v3 on v2

--- a/solution.py
+++ b/solution.py
@@ -69,7 +69,6 @@
 
 def kernel(
     x_hbm, b_hbm, c_hbm, step_hbm, rate_hbm, skip_hbm, taps_hbm, up_hbm, g_ref,
-    x_out, b_out, c_out, w_out, p_out,
     out_x, out_b, out_c, out_w, out_p,
     x_ref, b_ref, c_ref, step_ref, taps_ref, up_ref, rate_ref, skip_ref,
     halo, ext, pre, src, ws, wg, lead, trail,
@@ -78,10 +77,66 @@
     g_own, g_peer, gt,
     acc0, hold1, hold3, send2, relay, send1, send3, from_m, from_p, acc1, send_b, recv_b,
     part3, send_z, recv_z, grad_pre, w_row, w_y, w_z,
-    in_sem, out_sem, g_sem, ssem, rsem,
+    in_sem, g_sem, ssem, rsem,
 ):
     phase = Phases()
     phase("entry")
+    s = lax.axis_index("seq")
+    y = lax.axis_index("dp")
+    core = lax.rem(s, 2)
+    x = lax.rem(lax.div(s, 2), 4)
+    z = lax.div(s, ROW)
+    j = lax.rem(s, ROW)
+    sends, count = Counter(), Counter()
+    sent = []
+
+    def remote(source, target, to, index, slot):
+        return pltpu.make_async_remote_copy(
+            src_ref=source,
+            dst_ref=target,
+            send_sem=ssem.at[index],
+            recv_sem=rsem.at[slot],
+            device_id=to,
+            device_id_type=MESH,
+        )
+
+    def send(source, target, to, index, slot):
+        remote(source, target, to, index, slot).start()
+
+    def arrived(target, slot):
+        remote(target, target, (s, y), 0, slot).wait_recv()
+
+    def group(whole):
+        index = sends.take()
+        sent.append((whole, index))
+        return index
+
+    def row_mate(d):
+        other = lax.rem(j + d, ROW)
+        return other, (z * ROW + other, y)
+
+    def at_x(d):
+        return ((z * NX + lax.rem(x + d, NX)) * NC + core, y)
+
+    def at_y(d):
+        return (s, lax.rem(y + d, NY))
+
+    def at_z(d):
+        other = lax.rem(z + d, NZ)
+        return other, (other * ROW + j, y)
+
+    peer = (s + 1 - 2 * core, y)
+    following = (lax.rem(s + 1, NZ * ROW), y)
+    previous = (lax.rem(s + NZ * ROW - 1, NZ * ROW), y)
+
+    barrier = pltpu.get_barrier_semaphore()
+    partners = [at_z(d)[1] for d in (4, 3, 5, 2, 6, 1, 7)]
+    partners += [following, previous]
+    partners += [row_mate(d)[1] for d in range(1, ROW)]
+    partners += [at_y(d) for d in range(1, NY)]
+    for partner in partners:
+        pl.semaphore_signal(barrier, inc=1, device_id=partner, device_id_type=MESH)
+
     inputs = [
         pltpu.make_async_copy(source, target, in_sem.at[i])
         for i, (source, target) in enumerate(
@@ -91,72 +146,8 @@
             )
         )
     ]
-    outputs = [
-        pltpu.make_async_copy(source, target, out_sem.at[i])
-        for i, (source, target) in enumerate(
-            (
-                (out_x, x_out.at[0]), (out_b, b_out.at[0]), (out_c, c_out.at[0]),
-                (out_w, w_out), (out_p, p_out),
-            )
-        )
-    ]
     for copy in inputs:
         copy.start()
-    s = lax.axis_index("seq")
-    y = lax.axis_index("dp")
-    core = lax.rem(s, 2)
-    x = lax.rem(lax.div(s, 2), 4)
-    z = lax.div(s, ROW)
-    j = lax.rem(s, ROW)
-    sends, count = Counter(), Counter()
-    sent = []
-
-    def remote(source, target, to, index, slot):
-        return pltpu.make_async_remote_copy(
-            src_ref=source,
-            dst_ref=target,
-            send_sem=ssem.at[index],
-            recv_sem=rsem.at[slot],
-            device_id=to,
-            device_id_type=MESH,
-        )
-
-    def send(source, target, to, index, slot):
-        remote(source, target, to, index, slot).start()
-
-    def arrived(target, slot):
-        remote(target, target, (s, y), 0, slot).wait_recv()
-
-    def group(whole):
-        index = sends.take()
-        sent.append((whole, index))
-        return index
-
-    def row_mate(d):
-        other = lax.rem(j + d, ROW)
-        return other, (z * ROW + other, y)
-
-    def at_x(d):
-        return ((z * NX + lax.rem(x + d, NX)) * NC + core, y)
-
-    def at_y(d):
-        return (s, lax.rem(y + d, NY))
-
-    def at_z(d):
-        other = lax.rem(z + d, NZ)
-        return other, (other * ROW + j, y)
-
-    peer = (s + 1 - 2 * core, y)
-    following = (lax.rem(s + 1, NZ * ROW), y)
-    previous = (lax.rem(s + NZ * ROW - 1, NZ * ROW), y)
-
-    barrier = pltpu.get_barrier_semaphore()
-    partners = [row_mate(d)[1] for d in range(1, ROW)]
-    partners += [at_z(d)[1] for d in range(1, NZ)]
-    partners += [at_y(d) for d in range(1, NY)]
-    partners += [following, previous]
-    for partner in partners:
-        pl.semaphore_signal(barrier, inc=1, device_id=partner, device_id_type=MESH)
 
     @pl.loop(0, NZ * NX)
     def _(i):
@@ -166,6 +157,18 @@
     phase("inputs")
     for copy in inputs:
         copy.wait()
+
+    phase("barrier")
+    pl.semaphore_wait(barrier, len(partners))
+
+    phase("sends")
+    halo_at = count.take()
+    halo_out = remote(x_ref.at[pl.ds(TOK - 16, 16), :], halo, following, sends.take(), halo_at)
+    not_last, not_first = s < NZ * ROW - 1, s > 0
+
+    @pl.when(not_last)
+    def _():
+        halo_out.start()
 
     phase("decays")
     steps = step_ref[...]
@@ -195,18 +198,6 @@
         pieces[1, h] = grad_piece[h * HEAD_DIM : (h + 1) * HEAD_DIM]
     ext[0:16, :] = jnp.zeros((16, INNER), F32)
     ext[16:, :] = x_ref[...].astype(F32)
-
-    phase("barrier")
-    pl.semaphore_wait(barrier, len(partners))
-
-    phase("sends")
-    halo_at = count.take()
-    halo_out = remote(x_ref.at[pl.ds(TOK - 16, 16), :], halo, following, sends.take(), halo_at)
-    not_last, not_first = s < NZ * ROW - 1, s > 0
-
-    @pl.when(not_last)
-    def _():
-        halo_out.start()
 
     slot_j = [scan_slot(j, ROW, c) for c in range(NC)]
     my_slot = scan_slot(j, ROW, core)
@@ -485,8 +476,8 @@
                 send(send3.at[color, e], from_p.at[color, e], step_to(color, 3), three_out, three_at[color] + e)
 
     phase("maps")
-    out_b[...] = (loc_b[...] + dot(ws[...], end_grad, 1, 0)).astype(BF16)
-    out_c[...] = (loc_c[...] + dot(wg[...], start_state, 1, 0)).astype(BF16)
+    out_b[0] = (loc_b[...] + dot(ws[...], end_grad, 1, 0)).astype(BF16)
+    out_c[0] = (loc_c[...] + dot(wg[...], start_state, 1, 0)).astype(BF16)
 
     @pl.when(not_last)
     def _():
@@ -495,9 +486,7 @@
     value = jnp.zeros((TOK, INNER), F32)
     for tap in range(TAPS):
         value = value + taps_ref[tap : tap + 1, :] * grad_pre[tap : tap + TOK, :]
-    out_x[...] = value.astype(BF16)
-    for copy in outputs[:3]:
-        copy.start()
+    out_x[0] = value.astype(BF16)
 
     phase("taps_row")
     wy_at = count.take()
@@ -556,7 +545,6 @@
     for q in range(1, NZ):
         total = total + w_z[q]
     out_w[...] = total[0:TAPS] * SCALE
-    outputs[3].start()
 
     phase("stage3_wait")
     final = part3[z]
@@ -564,7 +552,6 @@
     for d in range(1, NZ):
         final = final + recv_z[d].astype(F32)
     out_p[...] = final
-    outputs[4].start()
 
     phase("drain")
     assert (sends.used, count.used) == (SENDS, ARRIVALS), (sends.used, count.used)
@@ -578,35 +565,28 @@
 
     for whole, index in sent:
         remote(whole, whole, (s, y), index, 0).wait_send()
-    for copy in outputs:
+    phase.open.close()
+
+
+def writer(*refs):
+    n = len(refs) // 2
+    copies = [pltpu.make_async_copy(refs[i], refs[n + i], refs[-1].at[i]) for i in range(n)]
+    for copy in copies:
+        copy.start()
+    for copy in copies:
         copy.wait()
-    phase.open.close()
-
-
-def writer(*refs):
-    n = (len(refs) - 2) // 3
-    taken, given, held, sems = refs[:n], refs[n : 2 * n], refs[2 * n : 3 * n], refs[3 * n :]
-    reads = [pltpu.make_async_copy(taken[i], held[i], sems[0].at[i]) for i in range(n)]
-    writes = [pltpu.make_async_copy(held[i], given[i], sems[1].at[i]) for i in range(n)]
-    for copy in reads:
-        copy.start()
-    for read, write in zip(reads, writes):
-        read.wait()
-        write.start()
-    for copy in writes:
-        copy.wait()
 
 
 SENDS, ARRIVALS = 28, 50
-VMEM_GRANT = 67043328
+VMEM_GRANT = 32 * 1024 * 1024
 
 
 def on_device(conv_input, in_map, out_map, step_size, decay_rate, skip_gain, conv_weight, grad_mixer, grad_output):
     hbm = pl.BlockSpec(memory_space=pltpu.HBM)
+    vmem = pl.BlockSpec(memory_space=pltpu.VMEM)
     piece = (HEAD_DIM, STATE)
     half = (TOK, 128)
     scratch = [
-        ((TOK, INNER), BF16), ((TOK, STATE), BF16), ((TOK, STATE), BF16), ((TAPS, INNER), F32), ((32, INNER), F32),
         ((TOK, INNER), BF16), ((TOK, STATE), BF16), ((TOK, STATE), BF16), ((HEADS, TOK), F32),
         ((TAPS, INNER), F32), ((TOK, INNER), BF16),
     ]
@@ -632,19 +612,24 @@
         jax.ShapeDtypeStruct((TAPS, INNER), F32),
         jax.ShapeDtypeStruct((32, INNER), F32),
     )
+    given = [
+        pltpu.with_memory_space_constraint(a, pltpu.HBM)
+        for a in (
+            conv_input, in_map, out_map, step_size[0].T, decay_rate, skip_gain, conv_weight, grad_mixer, grad_output
+        )
+    ]
     results = pl.pallas_call(
         kernel,
         name="mixer_backward",
         out_shape=outs,
         in_specs=[hbm] * 9,
-        out_specs=(hbm,) * 5,
+        out_specs=(vmem,) * 5,
         scratch_shapes=[
             *(pltpu.VMEM(shape, kind) for shape, kind in scratch),
             pltpu.SMEM((HEADS,), F32),
             pltpu.SMEM((HEADS,), F32),
             *(pltpu.VMEM(shape, kind) for shape, kind in scratch2),
             pltpu.SemaphoreType.DMA((8,)),
-            pltpu.SemaphoreType.DMA((5,)),
             pltpu.SemaphoreType.DMA((3,)),
             pltpu.SemaphoreType.DMA((SENDS,)),
             pltpu.SemaphoreType.DMA((ARRIVALS,)),
@@ -652,19 +637,15 @@
         compiler_params=pltpu.CompilerParams(
             collective_id=0, has_side_effects=True, vmem_limit_bytes=VMEM_GRANT
         ),
-    )(conv_input, in_map, out_map, step_size[0].T, decay_rate, skip_gain, conv_weight, grad_mixer, grad_output)
+    )(*given)
     return pl.pallas_call(
         writer,
         name="writer",
         out_shape=outs,
-        in_specs=[hbm] * 5,
+        in_specs=[vmem] * 5,
         out_specs=(hbm,) * 5,
-        scratch_shapes=[
-            *(pltpu.VMEM(out.shape, out.dtype) for out in outs),
-            pltpu.SemaphoreType.DMA((5,)),
-            pltpu.SemaphoreType.DMA((5,)),
-        ],
-        compiler_params=pltpu.CompilerParams(vmem_limit_bytes=VMEM_GRANT),
+        scratch_shapes=[pltpu.SemaphoreType.DMA((5,))],
+        compiler_params=pltpu.CompilerParams(vmem_limit_bytes=1024 * 1024),
     )(*results)
 
 

time: 51.4 us -> 50.2 us (0.977)
  Pallas kernels: 50.3 us -> 49 us
    pallas_call x1, Pallas kernels: 1.7 us -> 0.75 us  [on_device(): pl.pallas_call(writer, name='writer', out_shape=outs, in_specs=[vmem] * 5...]
where the time goes in v3:
time: 50.2 us; the launch traced here: 49.6 us
  Pallas kernels  49 us (98%)
  between operations  0.64 us (1%)
    pallas_call x1, Pallas kernels, on_device(): pl.pallas_call(kernel, name='mixer_backward', out_shape=outs, in_specs=[h...  48.2 us

profile of v3, /device:TPU:2, one launch (start us, length us, event | category | flops | bytes accessed | tf_op | source)
XLA Modules:
  0.0 49.6 jit_solution(3580406353600427633)
XLA Ops:
  0.6 48.2 %mixer_backward.1 = (bf16[1,256,256]{2,1,0:T(8,128)(2,1)S(1)}, bf16[1,256,128]{2,1,0:T(8,128)(2,1)S(1)}, bf16[1,256,128]{2,1,0:T(8,128)(2,1)S(1)}, f32[4,256]{1,0:T(4,128)S(1)}, f32[32,256]{1,0:T(8,128)S(1)}) custom-call(bf16[1,256,256]{2,1,0:T(8,128)(2,1)} %x_hbm.1, bf16[1,256,128]{2,1,0:T(8,128)(2,1)} %b_hbm.1, bf16[1,256,128]{2,1,0:T(8,128)(2,1)} %c_hbm.1, ...), custom_call_target="tpu_custom_call" | custom-call | tf_op jit(solution)/shard_map/mixer_backward/pallas_call | solution.py:621
  48.9 0.8 %writer.1 = (bf16[1,256,256]{2,1,0:T(8,128)(2,1)}, bf16[1,256,128]{2,1,0:T(8,128)(2,1)}, bf16[1,256,128]{2,1,0:T(8,128)(2,1)}, f32[4,256]{1,0:T(4,128)}, f32[32,256]{1,0:T(8,128)}) custom-call(bf16[1,256,256]{2,1,0:T(8,128)(2,1)S(1)} %get-tuple-element.10.refs_0_, bf16[1,256,128]{2,1,0:T(8,128)(2,1)S(1)} %get-tuple-element.11.refs_1_, ...), custom_call_target="tpu_custom_call" | custom-call | tf_op jit(solution)/shard_map/writer/pallas_call | solution.py:641

commit v4 on v3

--- a/solution.py
+++ b/solution.py
@@ -12,6 +12,7 @@
 BF16 = jnp.bfloat16
 
 NZ, NX, NC, NY = 8, 4, 2, 4
+FAR_Z, FAR_Y, FAR_ROW = (4, 3, 5, 2, 6, 1, 7), (2, 1, 3), (4, 3, 5, 2, 6, 7, 1)
 ROW = NX * NC
 HEADS, HEAD_DIM, STATE = 4, 64, 128
 TOK, INNER, TAPS = 256, 256, 4
@@ -75,7 +76,7 @@
     tot, pieces, row_p, row_t, prefix, row_sum, row_log, z_p, z_t, z_state, back, states,
     begun, loc_out, loc_src, loc_b, loc_c, mix, mix_peer,
     g_own, g_peer, gt,
-    acc0, hold1, hold3, send2, relay, send1, send3, from_m, from_p, acc1, send_b, recv_b,
+    acc0, hold1, hold3, send2, relay, send1, send3, came, acc1, send_b, recv_b,
     part3, send_z, recv_z, grad_pre, w_row, w_y, w_z,
     in_sem, g_sem, ssem, rsem,
 ):
@@ -130,7 +131,7 @@
     previous = (lax.rem(s + NZ * ROW - 1, NZ * ROW), y)
 
     barrier = pltpu.get_barrier_semaphore()
-    partners = [at_z(d)[1] for d in (4, 3, 5, 2, 6, 1, 7)]
+    partners = [at_z(d)[1] for d in FAR_Z]
     partners += [following, previous]
     partners += [row_mate(d)[1] for d in range(1, ROW)]
     partners += [at_y(d) for d in range(1, NY)]
@@ -204,7 +205,7 @@
     total_at = count.take()
     total_out = group(row_t.at[pl.ds(0, ROW - 1)])
     row_t[my_slot] = tot[...]
-    for d in range(1, ROW):
+    for d in FAR_ROW:
         other, to = row_mate(d)
         send(tot, row_t.at[scan_slot(j, ROW, lax.rem(other, 2))], to, total_out, total_at)
 
@@ -216,7 +217,7 @@
         def _():
             row_p[my_slot] = pieces[direction, x]
 
-        for d in range(NX):
+        for d in (*FAR_Y, 0):
             to_x = lax.rem(x + d, NX)
             copy = remote(
                 pieces.at[direction, to_x],
@@ -327,7 +328,7 @@
     my_z = scan_slot(z, NZ, core)
     zs_at = count.take(NZ - 1)
     zl_at = count.take(NZ - 1)
-    for d in range(1, NZ):
+    for d in FAR_Z:
         other, to = at_z(d)
         later = scan_slot(other, NZ, core) > my_z
         pair_of = [
@@ -370,7 +371,7 @@
     back_at = count.take()
     back_out = group(row_p.at[pl.ds(0, ROW - 1)])
     states[core, x] = back[my_slot]
-    for d in range(1, ROW):
+    for d in FAR_ROW:
         other, to = row_mate(d)
         send(back.at[scan_slot(other, ROW, core)], states.at[core, x], to, back_out, back_at)
 
@@ -419,16 +420,21 @@
     w_row[j] = jnp.concatenate(terms + [jnp.zeros((8 - TAPS, INNER), F32)], axis=0)
     w_at = count.take()
     w_out_at = group(w_row.at[pl.ds(0, ROW - 1)])
-    for d in range(1, ROW):
+    for d in FAR_ROW:
         send(w_row.at[j], w_row.at[j], row_mate(d)[1], w_out_at, w_at)
 
     axes = (at_x, at_y)
     far_at = [count.take(4) for _ in range(2)]
-    one_at = [count.take(4) for _ in range(2)]
-    three_at = [count.take(4) for _ in range(2)]
+    came_at = [count.take(4) for _ in range(2)]
     far_out, one_out, three_out = group(send2), group(send1), group(send3)
     def step_to(color, d):
         return axes[color](d)
+
+    def ahead(color, e):
+        send(send1.at[color, e], came.at[color, e, 0], step_to(color, 1), one_out, came_at[color] + e)
+
+    def behind(color, e):
+        send(send3.at[color, e], came.at[color, e, 1], step_to(color, 3), three_out, came_at[color] + e)
 
     def handle(color, d, e, part):
         if d == 0:
@@ -439,10 +445,12 @@
             send(send2.at[color, e], relay.at[color, e], to, far_out, far_at[color] + e)
         elif d == 1 and e not in PLUS:
             send1[color, e] = part.astype(BF16)
-            send(send1.at[color, e], from_m.at[color, e], step_to(color, 1), one_out, one_at[color] + e)
+            if e != 3:
+                ahead(color, e)
         elif d == 3 and e in PLUS:
             send3[color, e] = part.astype(BF16)
-            send(send3.at[color, e], from_p.at[color, e], step_to(color, 3), three_out, three_at[color] + e)
+            if e != 0:
+                behind(color, e)
         elif d == 1:
             hold1[color, PLUS.index(e)] = part
         else:
@@ -464,16 +472,20 @@
         handle(1, dy, dx, part[:, 128:])
 
     phase("relay")
-    for e in (2, 1, 0, 3):
+    for e in (2, 1, 3, 0):
         for color in range(2):
             arrived(relay.at[color, e], far_at[color] + e)
             got = relay[color, e].astype(F32)
             if e in PLUS:
                 send1[color, e] = (hold1[color, PLUS.index(e)] + got).astype(BF16)
-                send(send1.at[color, e], from_m.at[color, e], step_to(color, 1), one_out, one_at[color] + e)
+                ahead(color, e)
             else:
                 send3[color, e] = (hold3[color, MINUS.index(e)] + got).astype(BF16)
-                send(send3.at[color, e], from_p.at[color, e], step_to(color, 3), three_out, three_at[color] + e)
+                behind(color, e)
+            if e == 2:
+                ahead(color, 3)
+            elif e == 3:
+                behind(color, 0)
 
     phase("maps")
     out_b[0] = (loc_b[...] + dot(ws[...], end_grad, 1, 0)).astype(BF16)
@@ -496,7 +508,7 @@
     for q in range(1, ROW):
         total = total + w_row[q]
     w_y[y] = total
-    for d in range(1, NY):
+    for d in FAR_Y:
         send(w_y.at[y], w_y.at[y], at_y(d), wy_out, wy_at)
 
     phase("stage1_wait")
@@ -504,9 +516,8 @@
     second_out = group(send_b.at[:, pl.ds(1, 3)])
     for e in (2, 1, 3, 0):
         for color in range(2):
-            arrived(from_m.at[color, e], one_at[color] + e)
-            arrived(from_p.at[color, e], three_at[color] + e)
-            part = acc0[color, e] + from_m[color, e].astype(F32) + from_p[color, e].astype(F32)
+            arrived(came.at[color, e], came_at[color] + e)
+            part = acc0[color, e] + came[color, e, 0].astype(F32) + came[color, e, 1].astype(F32)
             if e == 0:
                 acc1[color] = part
             else:
@@ -521,7 +532,7 @@
     for q in range(1, NY):
         total = total + w_y[q]
     w_z[z] = total
-    for d in range(1, NZ):
+    for d in FAR_Z:
         send(w_z.at[z], w_z.at[z], at_z(d)[1], wz_out, wz_at)
 
     phase("stage2_wait")
@@ -535,7 +546,7 @@
             send_z[q, :, color * 128 : (color + 1) * 128] = part[q * 32 : (q + 1) * 32].astype(BF16)
     third_at = count.take()
     third_out = group(send_z.at[pl.ds(0, NZ - 1)])
-    for d in range(1, NZ):
+    for d in FAR_Z:
         other, to = at_z(d)
         send(send_z.at[other], recv_z.at[d], to, third_out, third_at)
 
@@ -577,7 +588,7 @@
         copy.wait()
 
 
-SENDS, ARRIVALS = 28, 50
+SENDS, ARRIVALS = 28, 42
 VMEM_GRANT = 32 * 1024 * 1024
 
 
@@ -600,8 +611,8 @@
         ((TOK, INNER), BF16), ((TOK, INNER), BF16),
         ((NZ * NX, TOK, 128), BF16), ((NZ * NX, TOK, 128), BF16), ((NX, NY, TOK, 2 * TOK), BF16),
         ((2, 4, *half), F32), ((2, 2, *half), F32), ((2, 2, *half), F32), ((2, 4, *half), BF16),
-        ((2, 4, *half), BF16), ((2, 4, *half), BF16), ((2, 4, *half), BF16), ((2, 4, *half), BF16),
-        ((2, 4, *half), BF16), ((2, *half), F32), ((2, 4, *half), BF16), ((2, 4, *half), BF16),
+        ((2, 4, *half), BF16), ((2, 4, *half), BF16), ((2, 4, *half), BF16), ((2, 4, 2, *half), BF16),
+        ((2, *half), F32), ((2, 4, *half), BF16), ((2, 4, *half), BF16),
         ((NZ, 32, INNER), F32), ((NZ, 32, INNER), BF16), ((NZ, 32, INNER), BF16),
         ((TOK + 8, INNER), F32), ((ROW, 8, INNER), F32), ((NY, 8, INNER), F32), ((NZ, 8, INNER), F32),
     ]

time: 50.2 us -> 48.5 us (0.966)
  Pallas kernels: 49 us -> 47.1 us
    pallas_call x1, Pallas kernels: 48.2 us -> 46.3 us  [on_device(): pl.pallas_call(kernel, name='mixer_backward', out_shape=outs, in_specs=[h...]
where the time goes in v4:
time: 48.5 us; the launch traced here: 47.7 us
  Pallas kernels  47.1 us (97%)
  between operations  0.64 us (1%)
    pallas_call x1, Pallas kernels, on_device(): pl.pallas_call(kernel, name='mixer_backward', out_shape=outs, in_specs=[h...  46.3 us

profile of v4, /device:TPU:2, one launch (start us, length us, event | category | flops | bytes accessed | tf_op | source)
XLA Modules:
  0.0 47.7 jit_solution(5042204020448944538)
XLA Ops:
  0.6 46.3 %mixer_backward.1 = (bf16[1,256,256]{2,1,0:T(8,128)(2,1)S(1)}, bf16[1,256,128]{2,1,0:T(8,128)(2,1)S(1)}, bf16[1,256,128]{2,1,0:T(8,128)(2,1)S(1)}, f32[4,256]{1,0:T(4,128)S(1)}, f32[32,256]{1,0:T(8,128)S(1)}) custom-call(bf16[1,256,256]{2,1,0:T(8,128)(2,1)} %x_hbm.1, bf16[1,256,128]{2,1,0:T(8,128)(2,1)} %b_hbm.1, bf16[1,256,128]{2,1,0:T(8,128)(2,1)} %c_hbm.1, ...), custom_call_target="tpu_custom_call" | custom-call | tf_op jit(solution)/shard_map/mixer_backward/pallas_call | solution.py:632
  47.0 0.8 %writer.1 = (bf16[1,256,256]{2,1,0:T(8,128)(2,1)}, bf16[1,256,128]{2,1,0:T(8,128)(2,1)}, bf16[1,256,128]{2,1,0:T(8,128)(2,1)}, f32[4,256]{1,0:T(4,128)}, f32[32,256]{1,0:T(8,128)}) custom-call(bf16[1,256,256]{2,1,0:T(8,128)(2,1)S(1)} %get-tuple-element.10.refs_0_, bf16[1,256,128]{2,1,0:T(8,128)(2,1)S(1)} %get-tuple-element.11.refs_1_, ...), custom_call_target="tpu_custom_call" | custom-call | tf_op jit(solution)/shard_map/writer/pallas_call | solution.py:652
